TPU v7x, 128 devices: a whole 4x4x4 slice. The times are simulated.
128 devices in a mesh: rows: 32 (over z, y, core), cols: 4 (over x).
Axes of the slice: x: 4, y: 4, z: 4, core: 2. Of those that a mesh axis runs over, the one named last changes fastest.
Arguments:
- features: bfloat16 [256, 512, 512], P('rows', 'cols'), may hold values from -6 to 6
- dw_weight: float32 [49, 512], replicated, may hold values from -0.875 to 0.875
- norm_gain: float32 [512], replicated, may hold values from 0.1 to 1.9
- w_up: bfloat16 [512, 2048], replicated, may hold values from -0.25 to 0.25
- w_down: bfloat16 [2048, 512], replicated, may hold values from -0.125 to 0.125
- cotangent: bfloat16 [256, 512, 512], P('rows', 'cols'), may hold values from -6 to 6
Outputs:
- grad_input: bfloat16 [256, 512, 512], P('rows', 'cols')
- grad_dw: float32 [49, 512], replicated
- grad_gain: float32 [512], replicated
- grad_up: float32 [512, 2048], replicated
- grad_down: float32 [2048, 512], replicated
All inputs are finite; a program needn't handle non-finite values.
Results may differ from a plain program's by a relative error of at most 0.019.
Values may be sent and summed in bfloat16 or wider, within the bound.
A program may use at most 128 MiB of HBM per device.

v0:
```python
import jax
import jax.numpy as jnp
from jax import lax
from jax.sharding import PartitionSpec as P

eps = 1e-06


def padded_2(block, sides, width):
    for axis, dim in sides:
        count = lax.axis_size(axis)
        forward = [(i, i + 1) for i in range(count - 1)]
        backward = [(target, source) for source, target in forward]
        low = lax.ppermute(
            lax.slice_in_dim(block, block.shape[dim] - width, None, axis=dim), axis, forward
        )
        high = lax.ppermute(lax.slice_in_dim(block, 0, width, axis=dim), axis, backward)
        block = jnp.concatenate([low, block, high], axis=dim)
    return block


def depthwise(padded, weight, rows, cols):
    total = jnp.zeros((rows, cols, padded.shape[2]), jnp.float32)
    for tap_i in range(7):
        for tap_j in range(7):
            total = (
                total
                + padded[tap_i : tap_i + rows, tap_j : tap_j + cols] * weight[7 * tap_i + tap_j]
            )
    return total


def pointwise(conv, gain, w_up, w_down, grad_out, keep):
    mean = jnp.mean(conv, axis=-1, keepdims=True)
    centred = conv - mean
    inv = lax.rsqrt(jnp.mean(centred * centred, axis=-1, keepdims=True) + eps)
    normed = centred * inv
    scaled = (normed * gain).astype(jnp.bfloat16)
    hidden = jnp.dot(scaled, w_up, preferred_element_type=jnp.float32)
    act = (0.5 * hidden * (1.0 + lax.erf(hidden * 0.7071067811865476))).astype(jnp.bfloat16)
    grad_kept = grad_out * keep.astype(jnp.bfloat16)
    grad_down = lax.dot_general(
        act, grad_kept, (((0,), (0,)), ((), ())), preferred_element_type=jnp.float32
    )
    grad_act = lax.dot_general(
        grad_out, w_down, (((1,), (1,)), ((), ())), preferred_element_type=jnp.float32
    )
    slope = (
        0.5 * (1.0 + lax.erf(hidden * 0.7071067811865476))
        + hidden * jnp.exp(-0.5 * hidden * hidden) * 0.3989422804014327
    )
    grad_hidden = (grad_act * slope).astype(jnp.bfloat16)
    hidden_kept = grad_hidden * keep.astype(jnp.bfloat16)
    grad_up = lax.dot_general(
        scaled, hidden_kept, (((0,), (0,)), ((), ())), preferred_element_type=jnp.float32
    )
    grad_scaled = lax.dot_general(
        grad_hidden, w_up, (((1,), (1,)), ((), ())), preferred_element_type=jnp.float32
    )
    grad_gain = jnp.sum(grad_scaled * normed * keep, axis=0)
    g_norm = grad_scaled * gain
    grad_conv = inv * (
        g_norm
        - jnp.mean(g_norm, axis=-1, keepdims=True)
        - normed * jnp.mean(g_norm * normed, axis=-1, keepdims=True)
    )
    return (grad_conv.astype(jnp.bfloat16), grad_up, grad_down, grad_gain)


def on_device(features, dw_weight, norm_gain, w_up, w_down, cotangent):
    rows, cols, chans = features.shape
    padded = padded_2(features, (("rows", 0), ("cols", 1)), 3).astype(jnp.float32)
    conv = depthwise(padded, dw_weight, rows, cols)
    keep = jnp.ones((rows * cols, 1), jnp.float32)
    grad_flat, grad_up, grad_down, grad_gain = pointwise(
        conv.reshape(rows * cols, chans),
        norm_gain,
        w_up,
        w_down,
        cotangent.reshape(rows * cols, chans),
        keep,
    )
    grad_conv = grad_flat.reshape(rows, cols, chans)
    grad_wide = padded_2(grad_conv, (("rows", 0), ("cols", 1)), 3)
    grad_f = grad_conv.astype(jnp.float32)
    taps = []
    for tap_i in range(7):
        for tap_j in range(7):
            taps.append(
                jnp.sum(padded[tap_i : tap_i + rows, tap_j : tap_j + cols] * grad_f, axis=(0, 1))
            )
    grad_dw = jnp.stack(taps)
    grad_pad = grad_wide.astype(jnp.float32)
    total = cotangent.astype(jnp.float32)
    for tap_i in range(7):
        for tap_j in range(7):
            total = (
                total
                + grad_pad[6 - tap_i : 6 - tap_i + rows, 6 - tap_j : 6 - tap_j + cols]
                * dw_weight[7 * tap_i + tap_j]
            )
    grad_input = total.astype(jnp.bfloat16)
    grad_up, grad_down, grad_dw, grad_gain = lax.psum(
        (grad_up, grad_down, grad_dw, grad_gain), ("rows", "cols")
    )
    return (grad_input, grad_dw, grad_gain, grad_up, grad_down)


def solution(mesh):
    return jax.shard_map(
        on_device,
        mesh=mesh,
        in_specs=(P("rows", "cols", None), P(), P(), P(), P(), P("rows", "cols", None)),
        out_specs=(P("rows", "cols", None), P(), P(), P(), P()),
        check_vma=False,
    )
```

profile of v0, /device:TPU:1, one launch (start us, length us, event | category | flops | bytes accessed | tf_op | source)
XLA Modules:
  0.0 328.7 jit_solution(11241434497956108759)
XLA Ops:
  7.2 0.0 copy-start
  7.2 0.0 copy-start.6
  7.2 0.0 all-reduce.3.cloned.1.call-start
  7.2 1.4 fusion.113
  8.6 4.6 %collective-permute-start = (bf16[3,128,512]{2,1,0:T(8,128)(2,1)S(1)}, bf16[3,128,512]{2,1,0:T(8,128)(2,1)S(1)}, u32[]{:S(2)}, u32[]{:S(2)}) collective-permute-start(bf16[3,128,512]{2,1,0:T(8,128)(2,1)S(1)} %get-tuple-element.70), channel_id=1, source_target_pairs={{0,4},{4,8},{8,12},{12,16},{16,20},{20,24},{24,28},{28,32},{32,36}... | collective-permute-start | bytes 1179656 | tf_op jit(solution)/shard_map/ppermute | solution.py:14
  13.2 1.9 collective-permute-start.1
  15.1 1.1 fusion.114
  16.2 0.0 copy-start.8
  16.3 0.0 copy-start.9
  16.3 0.0 copy-start.10
  16.3 0.0 copy-start.11
  16.3 0.0 copy-start.12
  16.4 1.2 fusion.115
  17.8 0.1 collective-permute-done
  17.9 0.0 copy-done.6
  17.9 0.1 constant_dynamic-update-slice_fusion.1
  18.0 4.5 %collective-permute-done.1 = bf16[3,128,512]{2,1,0:T(8,128)(2,1)S(1)} collective-permute-done((bf16[3,128,512]{2,1,0:T(8,128)(2,1)S(1)}, bf16[3,128,512]{2,1,0:T(8,128)(2,1)S(1)}, u32[]{:S(2)}, u32[]{:S(2)}) %collective-permute-start.1) | collective-permute-done | bytes 393248 | tf_op jit(solution)/shard_map/ppermute | solution.py:17
  22.7 1.3 collective-permute-start.3
  24.0 4.0 %collective-permute-start.2 = (bf16[14,3,512]{2,1,0:T(4,128)(2,1)S(1)}, bf16[14,3,512]{2,1,0:T(4,128)(2,1)S(1)}, u32[]{:S(2)}, u32[]{:S(2)}) collective-permute-start(bf16[14,3,512]{2,1,0:T(4,128)(2,1)S(1)} %get-tuple-element.65), channel_id=1, source_target_pairs={{0,1},{1,2},{2,3},{4,5},{5,6},{6,7},{8,9},{9,10},{10,11},{12,13},{... | collective-permute-start | bytes 129032 | tf_op jit(solution)/shard_map/ppermute | solution.py:14
  28.0 1.6 fusion.116
  29.6 0.0 collective-permute-done.3
  29.6 0.0 collective-permute-done.2
  29.6 2.5 maximum_convert_fusion
  32.1 0.0 copy-done.9
  32.5 54.0 %fusion.110 = (f32[8,128]{1,0:T(8,128)S(1)}, f32[8,128,512]{2,1,0:T(8,128)}) fusion(f32[512]{0:T(512)} %bitcast.48, f32[14,134,512]{2,1,0:T(8,128)} %maximum_convert_fusion, f32[512]{0:T(512)} %bitcast.47, f32[512]{0:T(512)S(1)} %bitcast.183, f32[512]{0:T(512)S(1)} %bitcast.185, f32[512]{0:T(512)S(1)} %bitcast.187, f32[512]{0:T(512)S(1)} %bitcast.189, ...), kind=kLoop, calls=%fused_computation.231 | loop fusion | flops 51379200 | bytes 104962048 | tf_op jit(solution)/shard_map/reduce_sum | solution.py:34
  86.5 0.0 copy-start.2
  86.5 0.0 copy-start.47
  86.5 2.1 multiply_reduce_fusion.2
  88.6 0.0 copy-done.2
  88.7 0.3 multiply_convert_fusion.3
  89.1 0.0 copy-start.4
  89.1 0.0 copy-start.7
  89.1 0.0 copy-start.48
  89.1 2.3 fusion.117
  91.5 5.0 %fusion.5 = bf16[1024,2048]{1,0:T(8,128)(2,1)S(1)} fusion(f32[1024,2048]{1,0:T(8,128)S(1)} %fusion.117, bf16[1024,512]{1,0:T(8,128)(2,1)S(1)} %bitcast.179, bf16[2048,512]{1,0:T(8,128)(2,1)S(1)} %copy-done.48), kind=kOutput, calls=%fused_computation.55 | convolution fusion | flops 2168455168 | bytes 15728640 | tf_op jit(solution)/shard_map/dot_general | solution.py:45
  96.5 0.0 copy-start.3
  96.6 0.0 copy-start.1
  96.6 3.4 %multiply_reduce_fusion = (f32[512]{0:T(512)}, f32[1024]{0:T(1024)S(1)}, f32[1024]{0:T(1024)S(1)}, f32[1024,512]{1,0:T(8,128)S(1)}) fusion(f32[8,128,512]{2,1,0:T(8,128)S(1)} %copy-done.2, f32[1024]{0:T(1024)S(1)} %get-tuple-element.121, f32[1024]{0:T(1024)S(1)} %rsqrt_bitcast_fusion, f32[512]{0:T(512)S(1)} %copy-done.47, ...), kind=kOutput, calls=%fused_computation.210 | convolution fusion | flops 2151675392 | bytes 10506240 | tf_op jit(solution)/shard_map/dot_general | solution.py:57
  99.9 0.0 copy-done.3
  99.9 0.2 copy-done.1
  100.2 6.6 %fusion.56 = (f32[512]{0:T(512)}, f32[512]{0:T(512)}, f32[512]{0:T(512)}, f32[512]{0:T(512)}, f32[512]{0:T(512)}, /*index=5*/f32[512]{0:T(512)}, f32[512]{0:T(51...) fusion(f32[14,134,512]{2,1,0:T(8,128)S(1)} %copy-done.1, ...), kind=kLoop, calls=%fused_computation.108 | loop fusion | flops 23583744 | bytes 43046912 | tf_op jit(solution)/shard_map/reduce_sum | solution.py:90
  106.8 1.0 fusion.112
  107.8 4.0 %fusion.20 = (f32[512]{0:T(512)}, f32[512]{0:T(512)}, f32[512]{0:T(512)}, f32[512]{0:T(512)}, f32[512]{0:T(512)}, /*index=5*/f32[512]{0:T(512)}, f32[512]{0:T(51...) fusion(f32[14,134,512]{2,1,0:T(8,128)S(1)} %copy-done.1, ...), kind=kLoop, calls=%fused_computation.72 | loop fusion | flops 14149120 | bytes 28338176 | tf_op jit(solution)/shard_map/reduce_sum | solution.py:90
  111.8 5.3 %fusion.38 = (f32[512]{0:T(512)}, f32[512]{0:T(512)}, f32[512]{0:T(512)}, f32[512]{0:T(512)}, f32[512]{0:T(512)}, /*index=5*/f32[512]{0:T(512)}, f32[512]{0:T(51...) fusion(f32[14,134,512]{2,1,0:T(8,128)S(1)} %copy-done.1, ...), kind=kLoop, calls=%fused_computation.90 | loop fusion | flops 19389440 | bytes 38834176 | tf_op jit(solution)/shard_map/reduce_sum | solution.py:90
  117.1 6.1 %fusion.6 = f32[2048,512]{1,0:T(8,128)} fusion(bf16[1024,512]{1,0:T(8,128)(2,1)S(1)} %bitcast.180, f32[1024,2048]{1,0:T(8,128)} %copy-done.49), kind=kOutput, calls=%fused_computation.58 | convolution fusion | flops 2157969408 | bytes 13631488 | tf_op jit(solution)/shard_map/dot_general | solution.py:42
  123.2 1.9 collective-permute-start.5
  125.1 3.6 %collective-permute-start.4 = (bf16[3,128,512]{2,1,0:T(8,128)(2,1)}, bf16[3,128,512]{2,1,0:T(8,128)(2,1)}, u32[]{:S(2)}, u32[]{:S(2)}) collective-permute-start(bf16[3,128,512]{2,1,0:T(8,128)(2,1)} %bitcast.53), channel_id=1, source_target_pairs={{0,4},{4,8},{8,12},{12,16},{16,20},{20,24},{24,28},{28,32},{32,36}... | collective-permute-start | bytes 1179656 | tf_op jit(solution)/shard_map/ppermute | solution.py:14
  128.8 9.4 %stack.199 = f32[49,512]{1,0:T(8,128)} concatenate(f32[1,512]{1,0:T(1,128)} %bitcast.315, f32[1,512]{1,0:T(1,128)} %bitcast.314, f32[1,512]{1,0:T(1,128)} %bitcast.313, f32[1,512]{1,0:T(1,128)} %bitcast.312, f32[1,512]{1,0:T(1,128)} %bitcast.311, f32[1,512]{1,0:T(1,128)} %bitcast.310, f32[1,512]{1,0:T(1,128)} %bitcast.309, f32[1,512]{1,0:T(1,128)} %bitcast.308, ...), dimensions={0} | concatenate | bytes 200704 | tf_op jit(solution)/shard_map/stack | solution.py:92
  138.1 6.9 %fusion.118 = f32[512,2048]{1,0:T(8,128)} fusion(bf16[1024,512]{1,0:T(8,128)(2,1)} %copy-done.4, bf16[1024,2048]{1,0:T(8,128)(2,1)} %copy-done.3), kind=kOutput, calls=%fused_computation.239 | convolution fusion | flops 2147483648 | bytes 9437184 | tf_op jit(solution)/shard_map/dot_general | solution.py:54
  145.0 0.0 all-reduce.3.cloned.1.call-update
  145.0 0.0 collective-permute-done.5
  145.1 0.0 collective-permute-done.4
  145.1 1.4 pad_maximum_fusion.2
  146.5 1.3 collective-permute-start.7
  147.8 4.6 %collective-permute-start.6 = (bf16[14,3,512]{2,1,0:T(4,128)(2,1)}, bf16[14,3,512]{2,1,0:T(4,128)(2,1)}, u32[]{:S(2)}, u32[]{:S(2)}) collective-permute-start(bf16[14,3,512]{2,1,0:T(4,128)(2,1)} %get-tuple-element.63), channel_id=1, source_target_pairs={{0,1},{1,2},{2,3},{4,5},{5,6},{6,7},{8,9},{9,10},{10,11},{12,13},{... | collective-permute-start | bytes 129032 | tf_op jit(solution)/shard_map/ppermute | solution.py:14
  152.4 70.5 %psum.29 = f32[512]{0:T(512)} all-reduce(f32[512]{0:T(512)} %get-tuple-element.54), channel_id=1, replica_groups=mesh['rows'=32,'cols'=4] {'rows','cols'}, use_global_device_ids=true, to_apply=%region_55.0 | all-reduce | flops 512 | bytes 4096 | tf_op jit(solution)/shard_map/psum | solution.py:103
  222.9 0.0 collective-permute-done.7
  222.9 0.0 collective-permute-done.6
  222.9 3.6 %maximum_convert_fusion.1 = f32[14,134,512]{2,1,0:T(8,128)} fusion(bf16[14,3,512]{2,1,0:T(4,128)(2,1)} %collective-permute-done.7, bf16[3,128,512]{2,1,0:T(8,128)(2,1)S(1)} %collective-permute-done.5, bf16[8,128,512]{2,1,0:T(8,128)(2,1)S(1)} %bitcast.178, bf16[3,128,512]{2,1,0:T(8,128)(2,1)} %collective-permute-done.4, ...), kind=kLoop, calls=%fused_computation.217 | loop fusion | flops 9605120 | bytes 5763072 | tf_op jit(solution)/shard_map/convert_element_type | solution.py:93
  226.5 52.3 %fusion.58 = bf16[8,128,512]{2,1,0:T(8,128)(2,1)} fusion(f32[14,134,512]{2,1,0:T(8,128)} %maximum_convert_fusion.1, bf16[8,128,512]{2,1,0:T(8,128)(2,1)} %param.11, f32[512]{0:T(512)} %bitcast.48, f32[512]{0:T(512)} %bitcast.47, f32[512]{0:T(512)S(1)} %bitcast.184, f32[512]{0:T(512)S(1)} %bitcast.186, f32[512]{0:T(512)S(1)} %bitcast.188, f32[512]{0:T(512)} %bitcast.190, ...), kind=kLoop, calls=%fused_computation.111 | loop fusion | flops 52428800 | bytes 104957952 | tf_op jit(solution)/shard_map/convert_element_type | solution.py:102
  278.7 34.7 %all-reduce.3.cloned.1.call-done = (f32[49,512]{1,0:T(8,128)}, f32[512,2048]{1,0:T(8,128)}, f32[2048,512]{1,0:T(8,128)}) async-done(((f32[49,512]{1,0:T(8,128)}, f32[512,2048]{1,0:T(8,128)}, f32[2048,512]{1,0:T(8,128)}), (f32[49,512]{1,0:T(8,128)}, f32[512,2048]{1,0:T(8,128)}, f32[2048,512]{1,0:T(8,128)})) %all-reduce.3.cloned.1.call-update) | async-done | bytes 8488976 | tf_op jit(solution)/shard_map/psum | solution.py:103
  313.4 1.6 copy.16
  315.0 4.8 %copy.17 = f32[512,2048]{1,0:T(8,128)} copy(f32[512,2048]{1,0:T(8,128)} %get-tuple-element.128) | data formatting | bytes 8388608
  319.8 2.0 copy.18
  (87 shorter events, 0.3 us)
Async XLA Ops:
  7.2 81.9 %copy-start = (bf16[512,2048]{1,0:T(8,128)(2,1)S(1)}, bf16[512,2048]{1,0:T(8,128)(2,1)}, u32[]{:S(2)}) copy-start(bf16[512,2048]{1,0:T(8,128)(2,1)} %param.9) | copy-start | bytes 6291460
  7.2 10.7 %copy-start.6 = (bf16[8,128,512]{2,1,0:T(8,128)(2,1)S(1)}, bf16[8,128,512]{2,1,0:T(8,128)(2,1)}, u32[]{:S(2)}) copy-start(bf16[8,128,512]{2,1,0:T(8,128)(2,1)} %param.6) | copy-start | bytes 3145732
  7.2 306.2 %all-reduce.3.cloned.1.call-start = ((), (), s32[]{:S(2)}) async-start(), calls=%async_computation | async-start | bytes 17006592 | tf_op jit(solution)/shard_map/psum | solution.py:103
  8.6 9.3 %collective-permute-start = (bf16[3,128,512]{2,1,0:T(8,128)(2,1)S(1)}, bf16[3,128,512]{2,1,0:T(8,128)(2,1)S(1)}, u32[]{:S(2)}, u32[]{:S(2)}) collective-permute-start(bf16[3,128,512]{2,1,0:T(8,128)(2,1)S(1)} %get-tuple-element.70), channel_id=1, source_target_pairs={{0,4},{4,8},{8,12},{12,16},{16,20},{20,24},{24,28},{28,32},{32,36}... | collective-permute-start | bytes 1179656 | tf_op jit(solution)/shard_map/ppermute | solution.py:14
  13.2 9.4 %collective-permute-start.1 = (bf16[3,128,512]{2,1,0:T(8,128)(2,1)S(1)}, bf16[3,128,512]{2,1,0:T(8,128)(2,1)S(1)}, u32[]{:S(2)}, u32[]{:S(2)}) collective-permute-start(bf16[3,128,512]{2,1,0:T(8,128)(2,1)S(1)} %get-tuple-element.69), channel_id=1, source_target_pairs={{4,0},{8,4},{12,8},{16,12},{20,16},{24,20},{28,24},{32,28},{36,32}... | collective-permute-start | bytes 1179656 | tf_op jit(solution)/shard_map/ppermute | solution.py:17
  16.2 15.9 %copy-start.8 = (f32[1,512]{1,0:T(1,128)}, f32[1,512]{1,0:T(1,128)S(1)}, u32[]{:S(2)}) copy-start(f32[1,512]{1,0:T(1,128)S(1)} %get-tuple-element.75) | copy-start | bytes 6148
  16.3 15.9 %copy-start.9 = (f32[1,512]{1,0:T(1,128)}, f32[1,512]{1,0:T(1,128)S(1)}, u32[]{:S(2)}) copy-start(f32[1,512]{1,0:T(1,128)S(1)} %get-tuple-element.76) | copy-start | bytes 6148
  16.3 15.9 %copy-start.10 = (f32[1,512]{1,0:T(1,128)}, f32[1,512]{1,0:T(1,128)S(1)}, u32[]{:S(2)}) copy-start(f32[1,512]{1,0:T(1,128)S(1)} %get-tuple-element.77) | copy-start | bytes 6148
  16.3 15.9 %copy-start.11 = (f32[1,512]{1,0:T(1,128)}, f32[1,512]{1,0:T(1,128)S(1)}, u32[]{:S(2)}) copy-start(f32[1,512]{1,0:T(1,128)S(1)} %get-tuple-element.78) | copy-start | bytes 6148
  16.3 15.9 %copy-start.12 = (f32[1,512]{1,0:T(1,128)}, f32[1,512]{1,0:T(1,128)S(1)}, u32[]{:S(2)}) copy-start(f32[1,512]{1,0:T(1,128)S(1)} %get-tuple-element.79) | copy-start | bytes 6148
  16.3 15.9 %copy-start.13 = (f32[1,512]{1,0:T(1,128)}, f32[1,512]{1,0:T(1,128)S(1)}, u32[]{:S(2)}) copy-start(f32[1,512]{1,0:T(1,128)S(1)} %get-tuple-element.80) | copy-start | bytes 6148
  16.3 15.9 %copy-start.14 = (f32[1,512]{1,0:T(1,128)}, f32[1,512]{1,0:T(1,128)S(1)}, u32[]{:S(2)}) copy-start(f32[1,512]{1,0:T(1,128)S(1)} %get-tuple-element.81) | copy-start | bytes 6148
  16.3 15.9 %copy-start.15 = (f32[1,512]{1,0:T(1,128)}, f32[1,512]{1,0:T(1,128)S(1)}, u32[]{:S(2)}) copy-start(f32[1,512]{1,0:T(1,128)S(1)} %get-tuple-element.82) | copy-start | bytes 6148
  16.3 15.9 %copy-start.16 = (f32[1,512]{1,0:T(1,128)}, f32[1,512]{1,0:T(1,128)S(1)}, u32[]{:S(2)}) copy-start(f32[1,512]{1,0:T(1,128)S(1)} %get-tuple-element.83) | copy-start | bytes 6148
  16.3 15.9 %copy-start.17 = (f32[1,512]{1,0:T(1,128)}, f32[1,512]{1,0:T(1,128)S(1)}, u32[]{:S(2)}) copy-start(f32[1,512]{1,0:T(1,128)S(1)} %get-tuple-element.84) | copy-start | bytes 6148
  16.3 15.9 %copy-start.18 = (f32[1,512]{1,0:T(1,128)}, f32[1,512]{1,0:T(1,128)S(1)}, u32[]{:S(2)}) copy-start(f32[1,512]{1,0:T(1,128)S(1)} %get-tuple-element.85) | copy-start | bytes 6148
  16.4 15.9 %copy-start.19 = (f32[1,512]{1,0:T(1,128)}, f32[1,512]{1,0:T(1,128)S(1)}, u32[]{:S(2)}) copy-start(f32[1,512]{1,0:T(1,128)S(1)} %get-tuple-element.86) | copy-start | bytes 6148
  16.4 15.9 %copy-start.20 = (f32[1,512]{1,0:T(1,128)}, f32[1,512]{1,0:T(1,128)S(1)}, u32[]{:S(2)}) copy-start(f32[1,512]{1,0:T(1,128)S(1)} %get-tuple-element.87) | copy-start | bytes 6148
  16.4 15.9 %copy-start.21 = (f32[1,512]{1,0:T(1,128)}, f32[1,512]{1,0:T(1,128)S(1)}, u32[]{:S(2)}) copy-start(f32[1,512]{1,0:T(1,128)S(1)} %get-tuple-element.88) | copy-start | bytes 6148
  16.4 15.9 %copy-start.22 = (f32[1,512]{1,0:T(1,128)}, f32[1,512]{1,0:T(1,128)S(1)}, u32[]{:S(2)}) copy-start(f32[1,512]{1,0:T(1,128)S(1)} %get-tuple-element.89) | copy-start | bytes 6148
  17.6 14.7 %copy-start.23 = (f32[1,512]{1,0:T(1,128)}, f32[1,512]{1,0:T(1,128)S(1)}, u32[]{:S(2)}) copy-start(f32[1,512]{1,0:T(1,128)S(1)} %get-tuple-element.90) | copy-start | bytes 6148
  17.6 14.7 %copy-start.24 = (f32[1,512]{1,0:T(1,128)}, f32[1,512]{1,0:T(1,128)S(1)}, u32[]{:S(2)}) copy-start(f32[1,512]{1,0:T(1,128)S(1)} %get-tuple-element.91) | copy-start | bytes 6148
  17.6 14.7 %copy-start.25 = (f32[1,512]{1,0:T(1,128)}, f32[1,512]{1,0:T(1,128)S(1)}, u32[]{:S(2)}) copy-start(f32[1,512]{1,0:T(1,128)S(1)} %get-tuple-element.92) | copy-start | bytes 6148
  17.6 14.7 %copy-start.26 = (f32[1,512]{1,0:T(1,128)}, f32[1,512]{1,0:T(1,128)S(1)}, u32[]{:S(2)}) copy-start(f32[1,512]{1,0:T(1,128)S(1)} %get-tuple-element.93) | copy-start | bytes 6148
  17.6 14.7 %copy-start.27 = (f32[1,512]{1,0:T(1,128)}, f32[1,512]{1,0:T(1,128)S(1)}, u32[]{:S(2)}) copy-start(f32[1,512]{1,0:T(1,128)S(1)} %get-tuple-element.94) | copy-start | bytes 6148
  17.6 14.7 %copy-start.28 = (f32[1,512]{1,0:T(1,128)}, f32[1,512]{1,0:T(1,128)S(1)}, u32[]{:S(2)}) copy-start(f32[1,512]{1,0:T(1,128)S(1)} %get-tuple-element.95) | copy-start | bytes 6148
  17.6 14.7 %copy-start.29 = (f32[1,512]{1,0:T(1,128)}, f32[1,512]{1,0:T(1,128)S(1)}, u32[]{:S(2)}) copy-start(f32[1,512]{1,0:T(1,128)S(1)} %get-tuple-element.96) | copy-start | bytes 6148
  17.6 14.7 %copy-start.30 = (f32[1,512]{1,0:T(1,128)}, f32[1,512]{1,0:T(1,128)S(1)}, u32[]{:S(2)}) copy-start(f32[1,512]{1,0:T(1,128)S(1)} %get-tuple-element.97) | copy-start | bytes 6148
  17.6 14.7 %copy-start.31 = (f32[1,512]{1,0:T(1,128)}, f32[1,512]{1,0:T(1,128)S(1)}, u32[]{:S(2)}) copy-start(f32[1,512]{1,0:T(1,128)S(1)} %get-tuple-element.98) | copy-start | bytes 6148
  17.7 14.7 %copy-start.32 = (f32[1,512]{1,0:T(1,128)}, f32[1,512]{1,0:T(1,128)S(1)}, u32[]{:S(2)}) copy-start(f32[1,512]{1,0:T(1,128)S(1)} %get-tuple-element.99) | copy-start | bytes 6148
  17.7 14.7 %copy-start.33 = (f32[1,512]{1,0:T(1,128)}, f32[1,512]{1,0:T(1,128)S(1)}, u32[]{:S(2)}) copy-start(f32[1,512]{1,0:T(1,128)S(1)} %get-tuple-element.100) | copy-start | bytes 6148
  17.7 14.7 %copy-start.34 = (f32[1,512]{1,0:T(1,128)}, f32[1,512]{1,0:T(1,128)S(1)}, u32[]{:S(2)}) copy-start(f32[1,512]{1,0:T(1,128)S(1)} %get-tuple-element.101) | copy-start | bytes 6148
  17.7 14.7 %copy-start.35 = (f32[1,512]{1,0:T(1,128)}, f32[1,512]{1,0:T(1,128)S(1)}, u32[]{:S(2)}) copy-start(f32[1,512]{1,0:T(1,128)S(1)} %get-tuple-element.102) | copy-start | bytes 6148
  17.7 14.7 %copy-start.36 = (f32[1,512]{1,0:T(1,128)}, f32[1,512]{1,0:T(1,128)S(1)}, u32[]{:S(2)}) copy-start(f32[1,512]{1,0:T(1,128)S(1)} %get-tuple-element.103) | copy-start | bytes 6148
  17.7 14.7 %copy-start.37 = (f32[1,512]{1,0:T(1,128)}, f32[1,512]{1,0:T(1,128)S(1)}, u32[]{:S(2)}) copy-start(f32[1,512]{1,0:T(1,128)S(1)} %get-tuple-element.104) | copy-start | bytes 6148
  17.7 14.7 %copy-start.38 = (f32[1,512]{1,0:T(1,128)}, f32[1,512]{1,0:T(1,128)S(1)}, u32[]{:S(2)}) copy-start(f32[1,512]{1,0:T(1,128)S(1)} %get-tuple-element.105) | copy-start | bytes 6148
  17.7 14.7 %copy-start.39 = (f32[1,512]{1,0:T(1,128)}, f32[1,512]{1,0:T(1,128)S(1)}, u32[]{:S(2)}) copy-start(f32[1,512]{1,0:T(1,128)S(1)} %get-tuple-element.106) | copy-start | bytes 6148
  17.7 14.7 %copy-start.40 = (f32[1,512]{1,0:T(1,128)}, f32[1,512]{1,0:T(1,128)S(1)}, u32[]{:S(2)}) copy-start(f32[1,512]{1,0:T(1,128)S(1)} %get-tuple-element.107) | copy-start | bytes 6148
  17.7 14.7 %copy-start.41 = (f32[1,512]{1,0:T(1,128)}, f32[1,512]{1,0:T(1,128)S(1)}, u32[]{:S(2)}) copy-start(f32[1,512]{1,0:T(1,128)S(1)} %get-tuple-element.108) | copy-start | bytes 6148
  22.7 6.9 %collective-permute-start.3 = (bf16[14,3,512]{2,1,0:T(4,128)(2,1)S(1)}, bf16[14,3,512]{2,1,0:T(4,128)(2,1)S(1)}, u32[]{:S(2)}, u32[]{:S(2)}) collective-permute-start(bf16[14,3,512]{2,1,0:T(4,128)(2,1)S(1)} %get-tuple-element.66), channel_id=1, source_target_pairs={{1,0},{2,1},{3,2},{5,4},{6,5},{7,6},{9,8},{10,9},{11,10},{13,12},{... | collective-permute-start | bytes 129032 | tf_op jit(solution)/shard_map/ppermute | solution.py:17
  24.0 5.6 %collective-permute-start.2 = (bf16[14,3,512]{2,1,0:T(4,128)(2,1)S(1)}, bf16[14,3,512]{2,1,0:T(4,128)(2,1)S(1)}, u32[]{:S(2)}, u32[]{:S(2)}) collective-permute-start(bf16[14,3,512]{2,1,0:T(4,128)(2,1)S(1)} %get-tuple-element.65), channel_id=1, source_target_pairs={{0,1},{1,2},{2,3},{4,5},{5,6},{6,7},{8,9},{9,10},{10,11},{12,13},{... | collective-permute-start | bytes 129032 | tf_op jit(solution)/shard_map/ppermute | solution.py:14
  29.5 2.9 copy-start.42
  29.5 2.9 copy-start.43
  29.5 2.9 copy-start.44
  29.6 2.9 copy-start.45
  29.6 2.9 copy-start.46
  86.5 2.2 copy-start.2
  86.5 2.2 copy-start.47
  89.1 2.4 copy-start.4
  89.1 2.4 copy-start.7
  89.1 2.4 copy-start.48
  91.5 5.1 %copy-start.49 = (f32[1024,2048]{1,0:T(8,128)}, f32[1024,2048]{1,0:T(8,128)S(1)}, u32[]{:S(2)}) copy-start(f32[1024,2048]{1,0:T(8,128)S(1)} %fusion.117) | copy-start | bytes 25165828
  96.5 3.4 %copy-start.3 = (bf16[1024,2048]{1,0:T(8,128)(2,1)}, bf16[1024,2048]{1,0:T(8,128)(2,1)S(1)}, u32[]{:S(2)}) copy-start(bf16[1024,2048]{1,0:T(8,128)(2,1)S(1)} %fusion.5) | copy-start | bytes 12582916
  96.6 3.6 %copy-start.1 = (f32[14,134,512]{2,1,0:T(8,128)S(1)}, f32[14,134,512]{2,1,0:T(8,128)}, u32[]{:S(2)}) copy-start(f32[14,134,512]{2,1,0:T(8,128)} %maximum_convert_fusion) | copy-start | bytes 11526148
  123.2 21.9 %collective-permute-start.5 = (bf16[3,128,512]{2,1,0:T(8,128)(2,1)}, bf16[3,128,512]{2,1,0:T(8,128)(2,1)S(1)}, u32[]{:S(2)}, u32[]{:S(2)}) collective-permute-start(bf16[3,128,512]{2,1,0:T(8,128)(2,1)} %bitcast.55), channel_id=1, source_target_pairs={{4,0},{8,4},{12,8},{16,12},{20,16},{24,20},{28,24},{32,28},{36,32}... | collective-permute-start | bytes 1179656 | tf_op jit(solution)/shard_map/ppermute | solution.py:17
  125.1 20.0 %collective-permute-start.4 = (bf16[3,128,512]{2,1,0:T(8,128)(2,1)}, bf16[3,128,512]{2,1,0:T(8,128)(2,1)}, u32[]{:S(2)}, u32[]{:S(2)}) collective-permute-start(bf16[3,128,512]{2,1,0:T(8,128)(2,1)} %bitcast.53), channel_id=1, source_target_pairs={{0,4},{4,8},{8,12},{12,16},{16,20},{20,24},{24,28},{28,32},{32,36}... | collective-permute-start | bytes 1179656 | tf_op jit(solution)/shard_map/ppermute | solution.py:14
  146.5 76.4 %collective-permute-start.7 = (bf16[14,3,512]{2,1,0:T(4,128)(2,1)}, bf16[14,3,512]{2,1,0:T(4,128)(2,1)}, u32[]{:S(2)}, u32[]{:S(2)}) collective-permute-start(bf16[14,3,512]{2,1,0:T(4,128)(2,1)} %get-tuple-element.64), channel_id=1, source_target_pairs={{1,0},{2,1},{3,2},{5,4},{6,5},{7,6},{9,8},{10,9},{11,10},{13,12},{... | collective-permute-start | bytes 129032 | tf_op jit(solution)/shard_map/ppermute | solution.py:17
  147.8 75.1 %collective-permute-start.6 = (bf16[14,3,512]{2,1,0:T(4,128)(2,1)}, bf16[14,3,512]{2,1,0:T(4,128)(2,1)}, u32[]{:S(2)}, u32[]{:S(2)}) collective-permute-start(bf16[14,3,512]{2,1,0:T(4,128)(2,1)} %get-tuple-element.63), channel_id=1, source_target_pairs={{0,1},{1,2},{2,3},{4,5},{5,6},{6,7},{8,9},{9,10},{10,11},{12,13},{... | collective-permute-start | bytes 129032 | tf_op jit(solution)/shard_map/ppermute | solution.py:14
  315.0 4.9 %copy-start.5 = (f32[2048,512]{1,0:T(8,128)S(1)}, f32[2048,512]{1,0:T(8,128)}, u32[]{:S(2)}) copy-start(f32[2048,512]{1,0:T(8,128)} %get-tuple-element.129) | copy-start | bytes 12582916
Sparse Core Ops, SparseCore 0:
  145.2 168.1 all-reduce.2
where the time goes:
time: 330 us; the launch traced here: 329 us
  other arithmetic  132 us (40%)
  blocking collectives  70.5 us (21%)
  waiting for transfers between devices  39.4 us (12%)
  local copies, waits for them, and re-layouts  24.7 us (7%)
  matrix products  23.8 us (7%)
  starting transfers between devices  23.3 us (7%)
  between operations  14.9 us (5%)
    psum x1, blocking collectives, on_device(): lax.psum((grad_up, grad_down, grad_dw, grad_gain), ('rows', 'cols'))  70.5 us
    reduce_sum x1, other arithmetic, pointwise(): mean = jnp.mean(conv, axis=-1, keepdims=True)  54 us
    convert_element_type x1, other arithmetic, on_device(): grad_input = total.astype(jnp.bfloat16)  52.3 us
    psum x1, waiting for transfers between devices, on_device(): lax.psum((grad_up, grad_down, grad_dw, grad_gain), ('rows', 'cols'))  34.7 us
    ppermute x4, starting transfers between devices, padded_2(): lax.ppermute(lax.slice_in_dim(block, block.shape[dim] - width, None, axis...  16.8 us
    reduce_sum x3, other arithmetic, on_device(): jnp.sum(padded[tap_i:tap_i + rows, tap_j:tap_j + cols] * grad_f, axis=(0,...  15.9 us
    another operation x1, local copies, waits for them, and re-layouts, on_device(): grad_dw = jnp.stack(taps)  9.37 us
    unnamed x105, local copies, waits for them, and re-layouts  9.05 us
  transfers between devices with their start and end apart: 9, of which 3 were waited for; matrix products, arithmetic and copies ran while one was open for 24% of the time, Pallas kernels for 0%

commit v1 on v0

v1 whole, which is shorter than its diff:
```python
import jax
import jax.numpy as jnp
from jax import lax
from jax.experimental import pallas as pl
from jax.experimental.pallas import tpu as pltpu
from jax.sharding import PartitionSpec as P

EPS = 1e-06
ROWS, COLS, CH, FF = 8, 128, 512, 2048
PIX = ROWS * COLS
NCH = 4
FC = FF // NCH
LEFT = 8
F32, BF16 = jnp.float32, jnp.bfloat16
MESH = pl.DeviceIdType.MESH
FIRST_AXIS = ((0, 2), (1, 0), (2, 1), (0, 2))
SIDES = ((-1, 0), (1, 0), (0, -1), (0, 1), (-1, -1), (-1, 1), (1, -1), (1, 1))
(R_CORE, R_A0, R_A1, R_B0, R_B1, R_PRS, R_PAG, R_G0, R_G1, R_H0, R_H1, R_CAG) = range(12)


def kernel(
    feat_hbm, dww_hbm, gain_hbm, wup_hbm, wdn_hbm, cot_hbm,
    gin_hbm, small_hbm, big_hbm,
    fbuf, cbuf, wup, wdn, dww, gainb, xf, gp, wb, cv, invb, sc, act, gh, gs, G, gb, obuf,
    scol, hrow, hcol, hcor,
    csend, crecv, M, axa, axs, axb, pls, plr, GA, GB,
    gd, dsm, drc, dps, dpr, dax, dga, dout,
    ld, hsend, hrecv, csem, rsem, ssend, srecv, osem,
):
    ra, ca = lax.axis_index("rows"), lax.axis_index("cols")
    core = ra % 2
    y, z, x = (ra // 2) % 4, ra // 8, ca

    def device(x_, y_, z_, core_):
        return ((z_ * 4 + y_) * 2 + core_, x_)

    partner = device(x, y, z, 1 - core)

    def side(dr, dc):
        return ((ra + dr + 32) % 32, (ca + dc + 4) % 4)

    def plane_peer(d, axis):
        ix, iy, iz = axis
        u, v = ix * y + iy * z + iz * x, ix * z + iy * x + iz * y
        u2, v2 = (u + d // 4) % 4, (v + d % 4) % 4
        return (
            device(
                ix * x + iy * v2 + iz * u2,
                ix * u2 + iy * y + iz * v2,
                ix * v2 + iy * u2 + iz * z,
                core,
            ),
            u2 * 4 + v2,
        )

    def plane_pos(axis):
        ix, iy, iz = axis
        return (ix * y + iy * z + iz * x) * 4 + ix * z + iy * x + iz * y

    def axis_of(c):
        a0, a1 = FIRST_AXIS[c]
        return tuple((a0 == n) * (1 - core) + (a1 == n) * core for n in range(3))

    def along(axis, step):
        ix, iy, iz = axis
        return device(
            (x + step * ix) % 4, (y + step * iy) % 4, (z + step * iz) % 4, core
        )

    def remote(src, dst, send, recv, to):
        return pltpu.make_async_remote_copy(
            src_ref=src, dst_ref=dst, send_sem=send, recv_sem=recv, device_id=to, device_id_type=MESH
        )

    def landed(ref, sem):
        pltpu.make_async_copy(ref, ref, sem).wait()

    loads = [
        pltpu.make_async_copy(s, d, ld.at[n])
        for n, (s, d) in enumerate(
            ((feat_hbm, fbuf), (dww_hbm, dww), (gain_hbm, gainb), (cot_hbm, cbuf), (wup_hbm, wup), (wdn_hbm, wdn))
        )
    ]
    for c_ in loads:
        c_.start()
    barrier = pltpu.get_barrier_semaphore()
    pl.semaphore_signal(barrier, inc=1, device_id=partner, device_id_type=MESH)
    for dr, dc in SIDES:
        pl.semaphore_signal(barrier, inc=1, device_id=side(dr, dc), device_id_type=MESH)
    for axis in ((1, 0, 0), (0, 1, 0), (0, 0, 1)):
        @pl.loop(1, 16)
        def _(d, axis=axis):
            pl.semaphore_signal(barrier, inc=1, device_id=plane_peer(d, axis)[0], device_id_type=MESH)

    for c_ in loads[:3]:
        c_.wait()

    def edges(pad, phase):
        for n, start in ((0, LEFT), (1, LEFT + COLS - 8)):
            for cc in range(4):
                scol[phase, n, :, :, cc * 128 : cc * 128 + 128] = pad[
                    cc, 3 : 3 + ROWS, start : start + 8, :
                ].astype(BF16)

    @pl.loop(0, ROWS)
    def _(r):
        for cc in range(4):
            xf[cc, 3 + r, LEFT : LEFT + COLS, :] = fbuf[r, :, cc * 128 : cc * 128 + 128].astype(F32)

    edges(xf, 0)
    pl.semaphore_wait(barrier, 1 + len(SIDES) + 45)

    def halo_copies(phase, rows_src):
        out = []
        for n, (dr, dc) in enumerate(SIDES):
            rs = slice(0, 3) if dr < 0 else slice(5, 8)
            if dc == 0:
                src, dst = rows_src.at[rs], hrow.at[phase, n]
            elif dr == 0:
                src, dst = scol.at[phase, n - 2], hcol.at[phase, n - 2]
            else:
                src, dst = scol.at[phase, 0 if dc < 0 else 1, rs], hcor.at[phase, n - 4]
            out.append(remote(src, dst, hsend.at[phase, n], hrecv.at[phase, n], side(dr, dc)))
        return out

    valid = {
        -1: jnp.where(ra < 31, 1.0, 0.0).astype(F32),
        1: jnp.where(ra > 0, 1.0, 0.0).astype(F32),
    }
    valid_c = {
        -1: jnp.where(ca < 3, 1.0, 0.0).astype(F32),
        1: jnp.where(ca > 0, 1.0, 0.0).astype(F32),
    }

    def halo_cols(phase, copies, pad):
        for n in (2, 3):
            copies[n].wait_recv()
            dc = SIDES[n][1]
            start = LEFT + COLS if dc < 0 else LEFT - 8
            for cc in range(4):
                pad[cc, 3 : 3 + ROWS, start : start + 8, :] = (
                    hcol[phase, n - 2, :, :, cc * 128 : cc * 128 + 128].astype(F32) * valid_c[dc]
                )

    def halo_rows(phase, copies, pad):
        for n in (0, 1):
            copies[n].wait_recv()
            dr = SIDES[n][0]
            r0 = 3 + ROWS if dr < 0 else 0
            for r in range(3):
                for cc in range(4):
                    pad[cc, r0 + r, LEFT : LEFT + COLS, :] = (
                        hrow[phase, n, r, :, cc * 128 : cc * 128 + 128].astype(F32) * valid[dr]
                    )
        for n in range(4, 8):
            copies[n].wait_recv()
            dr, dc = SIDES[n]
            r0 = 3 + ROWS if dr < 0 else 0
            start = LEFT + COLS if dc < 0 else LEFT - 8
            for cc in range(4):
                pad[cc, r0 : r0 + 3, start : start + 8, :] = hcor[
                    phase, n - 4, :, :, cc * 128 : cc * 128 + 128
                ].astype(F32) * (valid[dr] * valid_c[dc])

    def conv(pad, flip, cc, cb, inner):
        rhos = range(3, 11) if inner else (0, 1, 2, 11, 12, 13)
        rows = range(ROWS) if inner else (0, 1, 2, 5, 6, 7)
        base = cb * 32

        def at(r, b):
            return pl.ds(pl.multiple_of(r * COLS + base + 8 * b, 8), 8)

        def body(j, acc):
            acc = dict(zip([(r, b) for r in rows for b in range(4)], acc))
            w = [wb[cc, (48 - 7 * i - j) if flip else (7 * i + j)] for i in range(7)]
            for rho in rhos:
                for b in range(4):
                    v = pad[cc, rho, pl.ds(base + (8 * b + LEFT - 3) + j, 8), :]
                    for r in rows:
                        if 0 <= rho - r <= 6:
                            acc[r, b] = acc[r, b] + v * w[rho - r]
            return tuple(acc.values())

        if inner:
            start = tuple(jnp.zeros((8, 128), F32) for r in rows for b in range(4))
        else:
            start = tuple(cv[cc, at(r, b), :] for r in rows for b in range(4))
        acc = lax.fori_loop(0, 7, body, start)
        for n, (r, b) in enumerate([(r, b) for r in rows for b in range(4)]):
            cv[cc, at(r, b), :] = acc[n]

    halo = halo_copies(0, fbuf)
    for n in (2, 3, 0, 1, 4, 5, 6, 7):
        halo[n].start()

    for t in range(49):
        for cc in range(4):
            wb[cc, t] = jnp.broadcast_to(dww[t : t + 1, cc * 128 : cc * 128 + 128], (8, 128))

    @pl.loop(0, 8)
    def _(t):
        conv(xf, False, t // 2, 1 + t % 2, True)

    halo_cols(0, halo, xf)

    @pl.loop(0, 8)
    def _(t):
        conv(xf, False, t // 2, 3 * (t % 2), True)

    halo_rows(0, halo, xf)

    @pl.loop(0, 16)
    def _(t):
        conv(xf, False, t // 4, t % 4, False)

    @pl.loop(0, 16)
    def _(t):
        ps = pl.ds(pl.multiple_of(t * 64, 64), 64)
        v = [cv[cc, ps, :] for cc in range(4)]
        mean = jnp.sum(v[0] + v[1] + v[2] + v[3], axis=1, keepdims=True) * (1.0 / CH)
        v = [a - mean for a in v]
        sq = [a * a for a in v]
        inv = lax.rsqrt(jnp.sum(sq[0] + sq[1] + sq[2] + sq[3], axis=1, keepdims=True) * (1.0 / CH) + EPS)
        invb[ps, :] = jnp.broadcast_to(inv, (64, 128))
        for cc in range(4):
            n_ = v[cc] * inv
            cv[cc, ps, :] = n_
            sc[ps, cc * 128 : cc * 128 + 128] = (n_ * gainb[:, cc * 128 : cc * 128 + 128]).astype(BF16)

    for c_ in loads[3:]:
        c_.wait()

    def mlp_a(c, half):
        for pb in (2 * half, 2 * half + 1):
            ps = slice(pb * 256, pb * 256 + 256)
            h = jnp.dot(sc[ps, :], wup[:, c * FC : (c + 1) * FC], preferred_element_type=F32)
            ga = lax.dot_general(
                cbuf[ps, :], wdn[c * FC : (c + 1) * FC, :], (((1,), (1,)), ((), ())), preferred_element_type=F32
            )
            phi = 0.5 * (1.0 + lax.erf(h * 0.7071067811865476))
            act[ps, :] = (h * phi).astype(BF16)
            e = jnp.exp(-0.5 * h * h) * 0.3989422804014327
            gh[ps, :] = (ga * (phi + h * e)).astype(BF16)

    def put(c, slot, value):
        G[c, slot, 0] = value[:, 0:256]
        G[c, slot, 1] = value[:, 256:512]

    def mlp_down(c):
        put(c, core, lax.dot_general(act[...], cbuf[...], (((0,), (0,)), ((), ())), preferred_element_type=F32))

    def mlp_up(c):
        put(c, 1 - core, lax.dot_general(sc[...], gh[...], (((0,), (0,)), ((), ())), preferred_element_type=F32))

    def mlp_back(c):
        v = lax.dot_general(
            gh[...], wup[:, c * FC : (c + 1) * FC], (((1,), (1,)), ((), ())), preferred_element_type=F32
        )
        gs[...] = v if c == 0 else gs[...] + v

    def blocks(fn):
        @pl.loop(0, 8)
        def _(t):
            fn(t // 2, pl.ds((t % 2) * 8, 8), t)

    def st0(c):
        def go(a, n, t):
            rows = pl.ds(pl.multiple_of((t % 4) * 128, 128), 128)
            csend[c, a, n] = G[c, 1, t // 4, rows, :].reshape(8, 16, 256).astype(BF16)
        blocks(go)
        remote(csend.at[c], crecv.at[c], csem.at[c, R_CORE], rsem.at[c, R_CORE], partner).start()

    def st1(c):
        landed(crecv.at[c], rsem.at[c, R_CORE])
        axis = axis_of(c)
        p = axis[0] * x + axis[1] * y + axis[2] * z
        def go(a, n, t):
            rows = pl.ds(pl.multiple_of((t % 4) * 128, 128), 128)
            M[c, a, n] = (
                G[c, 0, t // 4, rows, :].reshape(8, 16, 256) + crecv[c, a, n].astype(F32)
            ).astype(BF16)
        blocks(go)
        far = (p + 2) % 4
        remote(M.at[c, far, 0:8], axa.at[c, 0], csem.at[c, R_A0], rsem.at[c, R_A0], along(axis, 1)).start()
        remote(M.at[c, far, 8:16], axa.at[c, 1], csem.at[c, R_A1], rsem.at[c, R_A1], along(axis, 3)).start()

    def st2(c):
        axis = axis_of(c)
        p = axis[0] * x + axis[1] * y + axis[2] * z
        landed(axa.at[c, 0], rsem.at[c, R_A0])
        landed(axa.at[c, 1], rsem.at[c, R_A1])
        right, left = (p + 1) % 4, (p + 3) % 4
        axs[c, 0, 0:8] = (M[c, right, 0:8].astype(F32) + axa[c, 0].astype(F32)).astype(BF16)
        axs[c, 0, 8:16] = M[c, right, 8:16]
        remote(axs.at[c, 0], axb.at[c, 0], csem.at[c, R_B0], rsem.at[c, R_B0], along(axis, 1)).start()
        axs[c, 1, 0:8] = M[c, left, 0:8]
        axs[c, 1, 8:16] = (M[c, left, 8:16].astype(F32) + axa[c, 1].astype(F32)).astype(BF16)
        remote(axs.at[c, 1], axb.at[c, 1], csem.at[c, R_B1], rsem.at[c, R_B1], along(axis, 3)).start()

    def st3(c):
        axis = axis_of(c)
        p = axis[0] * x + axis[1] * y + axis[2] * z
        landed(axb.at[c, 0], rsem.at[c, R_B0])
        landed(axb.at[c, 1], rsem.at[c, R_B1])
        pls[c] = (M[c, p].astype(F32) + axb[c, 0].astype(F32) + axb[c, 1].astype(F32)).astype(BF16)

        @pl.loop(1, 16)
        def _(d):
            to, pos = plane_peer(d, axis)
            remote(pls.at[c, pos], plr.at[c, d - 1], csem.at[c, R_PRS], rsem.at[c, R_PRS], to).start()

    def st4(c):
        axis = axis_of(c)
        p = axis[0] * x + axis[1] * y + axis[2] * z
        pos = plane_pos(axis)
        landed(plr.at[c], rsem.at[c, R_PRS])
        total = pls[c, pos].astype(F32)
        for d in range(15):
            total = total + plr[c, d].astype(F32)
        GA[c, p, pos] = total.astype(BF16)

        @pl.loop(1, 16)
        def _(d):
            to, _ = plane_peer(d, axis)
            remote(GA.at[c, p, pos], GA.at[c, p, pos], csem.at[c, R_PAG], rsem.at[c, R_PAG], to).start()

    def st5(c):
        axis = axis_of(c)
        p = axis[0] * x + axis[1] * y + axis[2] * z
        landed(plr.at[c], rsem.at[c, R_PAG])
        remote(GA.at[c, p], GA.at[c, p], csem.at[c, R_G0], rsem.at[c, R_G0], along(axis, 1)).start()
        remote(GA.at[c, p], GA.at[c, p], csem.at[c, R_G1], rsem.at[c, R_G1], along(axis, 3)).start()

    def st6(c):
        axis = axis_of(c)
        p = axis[0] * x + axis[1] * y + axis[2] * z
        right, left = (p + 1) % 4, (p + 3) % 4
        landed(GA.at[c, left], rsem.at[c, R_G0])
        landed(GA.at[c, right], rsem.at[c, R_G1])
        a = GA.at[c, left, 0:8]
        b = GA.at[c, right, 8:16]
        remote(a, a, csem.at[c, R_H0], rsem.at[c, R_H0], along(axis, 1)).start()
        remote(b, b, csem.at[c, R_H1], rsem.at[c, R_H1], along(axis, 3)).start()

    def st7(c):
        landed(axa.at[c, 0], rsem.at[c, R_H0])
        landed(axa.at[c, 1], rsem.at[c, R_H1])
        remote(GA.at[c], GB.at[c], csem.at[c, R_CAG], rsem.at[c, R_CAG], partner).start()
        pltpu.make_async_copy(GA.at[c], big_hbm.at[core, c], osem.at[2 * c]).start()

    def st8(c):
        landed(GB.at[c], rsem.at[c, R_CAG])
        pltpu.make_async_copy(GB.at[c], big_hbm.at[1 - core, c], osem.at[2 * c + 1]).start()

    def ln_back(quarter):
        def body(t, part):
            ps = pl.ds(pl.multiple_of(quarter * 256 + t * 64, 64), 64)
            inv = invb[ps, :]
            nv = [cv[cc, ps, :] for cc in range(4)]
            gv = [gs[ps, cc * 128 : cc * 128 + 128] for cc in range(4)]
            prod = [g * n for g, n in zip(gv, nv)]
            part = tuple(
                q + jnp.sum(pr.reshape(8, 8, 128), axis=0) for q, pr in zip(part, prod)
            )
            gains = [gainb[:, cc * 128 : cc * 128 + 128] for cc in range(4)]
            gn = [g * k for g, k in zip(gv, gains)]
            gm = [pr * k for pr, k in zip(prod, gains)]
            m1 = jnp.sum(gn[0] + gn[1] + gn[2] + gn[3], axis=1, keepdims=True) * (1.0 / CH)
            m2 = jnp.sum(gm[0] + gm[1] + gm[2] + gm[3], axis=1, keepdims=True) * (1.0 / CH)
            r, c0 = 2 * quarter + t // 2, (t % 2) * 64
            for cc in range(4):
                g = (inv * (gn[cc] - m1 - nv[cc] * m2)).astype(BF16)
                gb[r, pl.ds(pl.multiple_of(c0, 64), 64), cc * 128 : cc * 128 + 128] = g
                gp[cc, 3 + r, pl.ds(pl.multiple_of(LEFT + c0, 8), 64), :] = g.astype(F32)
            return part

        part = lax.fori_loop(0, 4, body, tuple(jnp.zeros((8, 128), F32) for _ in range(4)))
        for cc in range(4):
            row = jnp.sum(part[cc], axis=0, keepdims=True)
            gd[cc, 49:50, :] = row if quarter == 0 else gd[cc, 49:50, :] + row

    back = halo_copies(1, gb)

    def send_back():
        edges(gp, 1)
        for n in (0, 1, 2, 3, 4, 5, 6, 7):
            back[n].start()

    def gdw(cc, js):
        @pl.loop(js[0], js[1])
        def _(j):
            def body(cb, acc):
                acc = list(acc)
                base = cb * 64
                for b in range(8):
                    gv = [gp[cc, 3 + r, pl.ds(pl.multiple_of(base + LEFT + 8 * b, 8), 8), :] for r in range(8)]
                    for rho in range(14):
                        v = xf[cc, rho, pl.ds(base + (8 * b + LEFT - 3) + j, 8), :]
                        for r in range(max(0, rho - 6), min(8, rho + 1)):
                            acc[rho - r] = acc[rho - r] + v * gv[r]
                return tuple(acc)

            acc = lax.fori_loop(0, 2, body, tuple(jnp.zeros((8, 128), F32) for _ in range(7)))
            for i in range(7):
                gd[cc, pl.ds(7 * i + j, 1), :] = jnp.sum(acc[i], axis=0, keepdims=True)

    zaxis = (0, 0, 1)
    zpos = plane_pos(zaxis)

    def sm0():
        for cc in range(4):
            for tb in range(4):
                dsm[4 * cc + tb] = gd[cc, 16 * tb : 16 * tb + 16, :]
        remote(dsm, drc, ssend.at[0], srecv.at[0], partner).start()

    def sm1():
        landed(drc, srecv.at[0])
        dps[...] = dsm[...] + drc[...]

        @pl.loop(1, 16)
        def _(d):
            to, pos = plane_peer(d, zaxis)
            remote(dps.at[pos], dpr.at[d - 1], ssend.at[1], srecv.at[1], to).start()

    def sm2():
        landed(dpr, srecv.at[1])
        total = dps[zpos]
        for d in range(15):
            total = total + dpr[d]
        dax[z] = total
        for step in (1, 2, 3):
            remote(dax.at[z], dax.at[z], ssend.at[2], srecv.at[2], along(zaxis, step)).start()

    def sm3():
        landed(dpr.at[0:3], srecv.at[2])
        dga[zpos] = dax[0] + dax[1] + dax[2] + dax[3]

        @pl.loop(1, 16)
        def _(d):
            to, _ = plane_peer(d, zaxis)
            remote(dga.at[zpos], dga.at[zpos], ssend.at[3], srecv.at[3], to).start()

    def sm4():
        landed(dpr, srecv.at[3])
        for cc in range(4):
            for tb in range(4):
                dout[16 * tb : 16 * tb + 16, cc * 128 : cc * 128 + 128] = dga[4 * cc + tb]
        pltpu.make_async_copy(dout, small_hbm, osem.at[8]).start()

    def gin_inner(part, pair):
        @pl.loop(0, 4)
        def _(t):
            conv(gp, True, t, (1 + part) if pair == 0 else 3 * part, True)

    def gin_outer(cb):
        @pl.loop(0, 4)
        def _(t):
            conv(gp, True, t, cb, False)

    def gin_store(part):
        @pl.loop(part * 8, part * 8 + 8)
        def _(t):
            ps = pl.ds(pl.multiple_of(t * 64, 64), 64)
            for cc in range(4):
                cs = slice(cc * 128, cc * 128 + 128)
                obuf[ps, cs] = (cbuf[ps, cs].astype(F32) + cv[cc, ps, :]).astype(BF16)
        rows = slice(part * 512, part * 512 + 512)
        pltpu.make_async_copy(obuf.at[rows], gin_hbm.at[rows], osem.at[9 + part]).start()

    work = []
    chains = {}
    for c in range(NCH):
        work += [(0.75, lambda c=c: mlp_a(c, 0), None), (0.75, lambda c=c: mlp_a(c, 1), None)]
        work += [(0.62, lambda c=c: mlp_down(c), None), (0.62, lambda c=c: mlp_up(c), c)]
        work += [(0.62, lambda c=c: mlp_back(c), None)]
        chains[c] = list(
            zip((0.0, 1.8, 2.8, 4.0, 6.0, 6.0, 4.0, 2.8, 1.8), [lambda s=s, c=c: s(c) for s in (st0, st1, st2, st3, st4, st5, st6, st7, st8)])
        )
    work += [(0.4, lambda q=q: ln_back(q), None) for q in range(4)]
    work += [(0.2, send_back, None)]
    for cc in range(4):
        work += [(1.1, lambda cc=cc: gdw(cc, (0, 4)), None)]
        work += [(0.9, lambda cc=cc: gdw(cc, (4, 7)), "small" if cc == 3 else None)]
    chains["small"] = list(zip((0.0, 1.5, 6.5, 3.5, 6.5), (sm0, sm1, sm2, sm3, sm4)))
    work += [(1.7, lambda: gin_inner(0, 0), None), (1.7, lambda: gin_inner(1, 0), None)]
    work += [(0.1, lambda: halo_cols(1, back, gp), None)]
    work += [(1.7, lambda: gin_inner(0, 1), None), (1.7, lambda: gin_inner(1, 1), None)]
    work += [(0.3, lambda: halo_rows(1, back, gp), None)]
    work += [(0.55, lambda cb=cb: gin_outer(cb), None) for cb in range(4)]
    work += [(0.2, lambda: gin_store(0), None), (0.2, lambda: gin_store(1), None)]

    now = 0.0
    due = []

    def serve(limit):
        nonlocal now
        while due and (limit is None or min(due)[0] <= limit):
            when, key, n = min(due)
            due.remove((when, key, n))
            now = max(now, when) + 0.1
            chains[key][n][1]()
            if n + 1 < len(chains[key]):
                due.append((now + chains[key][n + 1][0], key, n + 1))

    for cost, fn, opens in work:
        fn()
        now += cost
        if opens is not None:
            due.append((now, 9 if opens == "small" else opens, 0))
            if opens == "small":
                chains[9] = chains["small"]
        serve(now)
    serve(None)

    for phase in (0, 1):
        for c_ in (halo, back)[phase]:
            c_.wait_send()
    for c in range(NCH):
        landed(csend.at[c], csem.at[c, R_CORE])
        landed(axa.at[c, 0], csem.at[c, R_A0])
        landed(axa.at[c, 1], csem.at[c, R_A1])
        landed(axb.at[c, 0], csem.at[c, R_B0])
        landed(axb.at[c, 1], csem.at[c, R_B1])
        landed(plr.at[c], csem.at[c, R_PRS])
        landed(plr.at[c], csem.at[c, R_PAG])
        landed(axb.at[c, 0], csem.at[c, R_G0])
        landed(axb.at[c, 1], csem.at[c, R_G1])
        landed(axa.at[c, 0], csem.at[c, R_H0])
        landed(axa.at[c, 1], csem.at[c, R_H1])
        landed(GA.at[c], csem.at[c, R_CAG])
        pltpu.make_async_copy(GA.at[c], big_hbm.at[core, c], osem.at[2 * c]).wait()
        pltpu.make_async_copy(GB.at[c], big_hbm.at[1 - core, c], osem.at[2 * c + 1]).wait()
    landed(dsm, ssend.at[0])
    landed(dpr, ssend.at[1])
    landed(dpr.at[0:3], ssend.at[2])
    landed(dpr, ssend.at[3])
    pltpu.make_async_copy(dout, small_hbm, osem.at[8]).wait()
    for part in (0, 1):
        rows = slice(part * 512, part * 512 + 512)
        pltpu.make_async_copy(obuf.at[rows], gin_hbm.at[rows], osem.at[9 + part]).wait()


def on_device(features, dw_weight, norm_gain, w_up, w_down, cotangent):
    vm, dma = pltpu.VMEM, pltpu.SemaphoreType.DMA
    any_ = pl.BlockSpec(memory_space=pl.ANY)
    gin, small, big = pl.pallas_call(
        kernel,
        out_shape=(
            jax.ShapeDtypeStruct((PIX, CH), BF16),
            jax.ShapeDtypeStruct((64, CH), F32),
            jax.ShapeDtypeStruct((2, NCH, 4, 16, 16, 256), BF16),
        ),
        in_specs=[any_] * 6,
        out_specs=[any_] * 3,
        scratch_shapes=[
            vm((ROWS, COLS, CH), BF16), vm((PIX, CH), BF16), vm((CH, FF), BF16), vm((FF, CH), BF16),
            vm((49, CH), F32), vm((1, CH), F32),
            vm((4, 14, 144, 128), F32), vm((4, 14, 144, 128), F32), vm((4, 49, 8, 128), F32),
            vm((4, PIX, 128), F32), vm((PIX, 128), F32), vm((PIX, CH), BF16),
            vm((PIX, FC), BF16), vm((PIX, FC), BF16), vm((PIX, CH), F32),
            vm((NCH, 2, 2, 512, 256), F32), vm((ROWS, COLS, CH), BF16), vm((PIX, CH), BF16),
            vm((2, 2, 8, 8, CH), BF16), vm((2, 2, 3, COLS, CH), BF16), vm((2, 2, 8, 8, CH), BF16), vm((2, 4, 3, 8, CH), BF16),
            vm((NCH, 4, 16, 16, 256), BF16), vm((NCH, 4, 16, 16, 256), BF16), vm((NCH, 4, 16, 16, 256), BF16),
            vm((NCH, 2, 8, 16, 256), BF16), vm((NCH, 2, 16, 16, 256), BF16), vm((NCH, 2, 16, 16, 256), BF16),
            vm((NCH, 16, 16, 256), BF16), vm((NCH, 15, 16, 256), BF16),
            vm((NCH, 4, 16, 16, 256), BF16), vm((NCH, 4, 16, 16, 256), BF16),
            vm((4, 64, 128), F32), vm((16, 16, 128), F32), vm((16, 16, 128), F32), vm((16, 16, 128), F32),
            vm((15, 16, 128), F32), vm((4, 16, 128), F32), vm((16, 16, 128), F32), vm((64, CH), F32),
            dma((6,)), dma((2, 8)), dma((2, 8)), dma((NCH, 12)), dma((NCH, 12)), dma((4,)), dma((4,)), dma((11,)),
        ],
        compiler_params=pltpu.CompilerParams(
            collective_id=0, has_side_effects=True, vmem_limit_bytes=66_000_000
        ),
        name="block_backward",
    )(features, dw_weight, norm_gain.reshape(1, CH), w_up, w_down, cotangent.reshape(PIX, CH))
    big = big.reshape(2, NCH, 2, 512, 256)
    grad_down = big[0].transpose(0, 2, 1, 3).reshape(FF, CH).astype(F32)
    grad_up = big[1].transpose(2, 0, 1, 3).reshape(CH, FF).astype(F32)
    return gin.reshape(ROWS, COLS, CH), small[:49], small[49], grad_up, grad_down


def solution(mesh):
    return jax.shard_map(
        on_device,
        mesh=mesh,
        in_specs=(P("rows", "cols", None), P(), P(), P(), P(), P("rows", "cols", None)),
        out_specs=(P("rows", "cols", None), P(), P(), P(), P()),
        check_vma=False,
    )
```

time: 330 us -> 110 us (0.33)
  other arithmetic: 132 us -> 0.75 us
  Pallas kernels: 0 us -> 84.2 us
  blocking collectives: 70.5 us -> 0 us
  waiting for transfers between devices: 39.4 us -> 0 us
  matrix products: 23.8 us -> 0 us
  starting transfers between devices: 23.3 us -> 0 us
  between operations: 14.9 us -> 0.68 us
    pallas_call x0 -> x1, Pallas kernels: none -> 84.2 us  [on_device(): pl.pallas_call(kernel, out_shape=(jax.ShapeDtypeStruct((PIX, CH), BF16),...]
    reduce_sum x5 -> x0, other arithmetic: 72 us -> none  [the longest x1 54 us: pointwise(): mean = jnp.mean(conv, axis=-1, keepdims=True)]
    psum x1 -> x0, blocking collectives: 70.5 us -> none  [on_device(): lax.psum((grad_up, grad_down, grad_dw, grad_gain), ('rows', 'cols'))]
    convert_element_type x4 -> x2, other arithmetic: 58.7 us -> 0.75 us  [the longest x1 0.38 us: on_device(): grad_up = big[1].transpose(2, 0, 1, 3).reshape(CH, FF).astype(F32)]
    psum x1 -> x0, waiting for transfers between devices: 34.7 us -> none  [on_device(): lax.psum((grad_up, grad_down, grad_dw, grad_gain), ('rows', 'cols'))]
    dot_general x5 -> x0, matrix products: 23.8 us -> none  [the longest x1 6.9 us: pointwise(): lax.dot_general(scaled, hidden_kept, (((0,), (0,)), ((), ())), preferred_...]
    ppermute x8 -> x0, starting transfers between devices: 23.2 us -> none  [the longest x4 16.8 us: padded_2(): lax.ppermute(lax.slice_in_dim(block, block.shape[dim] - width, None, axis...]
    convert_element_type x0 -> x3, local copies, waits for them, and re-layouts: none -> 14.9 us  [the longest x2 11.7 us: on_device(): grad_up = big[1].transpose(2, 0, 1, 3).reshape(CH, FF).astype(F32)]
  transfers between devices with their start and end apart: 9 -> 0, of which waited for: 3 -> 0; matrix products, arithmetic and copies ran while one was open for 24% -> 0% of each run, Pallas kernels for 0% -> 0%
where the time goes in v1:
time: 110 us; the launch traced here: 109 us
  Pallas kernels  84.2 us (77%)
  local copies, waits for them, and re-layouts  23.7 us (22%)
    pallas_call x1, Pallas kernels, on_device(): pl.pallas_call(kernel, out_shape=(jax.ShapeDtypeStruct((PIX, CH), BF16),...  84.2 us
    convert_element_type x2, local copies, waits for them, and re-layouts, on_device(): grad_up = big[1].transpose(2, 0, 1, 3).reshape(CH, FF).astype(F32)  11.7 us
    unnamed x4, local copies, waits for them, and re-layouts  3.43 us
    convert_element_type x1, local copies, waits for them, and re-layouts, on_device(): grad_down = big[0].transpose(0, 2, 1, 3).reshape(FF, CH).astype(F32)  3.24 us
    slice x1, local copies, waits for them, and re-layouts, on_device(): grad_down = big[0].transpose(0, 2, 1, 3).reshape(FF, CH).astype(F32)  2.52 us

profile of v1, /device:TPU:1, one launch (start us, length us, event | category | flops | bytes accessed | tf_op | source)
XLA Modules:
  0.0 109.3 jit_solution(5422168755068114107)
XLA Ops:
  0.6 84.2 %block_backward.1 = (bf16[1024,512]{1,0:T(8,128)(2,1)}, f32[64,512]{1,0:T(8,128)}, bf16[2,4,4,16,16,256]{5,4,3,2,1,0:T(8,128)(2,1)}) custom-call(bf16[8,128,512]{2,1,0:T(8,128)(2,1)} %feat_hbm.1, f32[49,512]{1,0:T(8,128)} %dww_hbm.1, f32[1,512]{1,0:T(1,128)} %bitcast.21, bf16[512,2048]{1,0:T(8,128)(2,1)} %wup_hbm.1, bf16[2048,512]{1,0:T(8,128)(2,1)} %wdn_hbm.1, ...), custom_call_target="tpu_custom_call" | custom-call | tf_op jit(solution)/shard_map/block_backward/pallas_call | solution.py:546
  84.8 1.3 %slice.15 = f32[1,512]{1,0:T(1,128)} slice(f32[64,512]{1,0:T(8,128)} %get-tuple-element.9), slice={[49:50], [0:512]} | slice | bytes 4096 | tf_op jit(solution)/shard_map/slice | solution.py:579
  86.1 1.6 %slice.14 = f32[49,512]{1,0:T(8,128)} slice(f32[64,512]{1,0:T(8,128)} %get-tuple-element.9), slice={[0:49], [0:512]} | slice | bytes 200704 | tf_op jit(solution)/shard_map/slice | solution.py:579
  87.7 2.5 %fusion = (bf16[1,4,4,16,16,256]{5,4,3,2,1,0:T(8,128)(2,1)S(1)}, bf16[1,4,4,16,16,256]{5,4,3,2,1,0:T(8,128)(2,1)S(1)}) fusion(bf16[2,4,4,16,16,256]{5,4,3,2,1,0:T(8,128)(2,1)} %get-tuple-element.10), kind=kLoop, calls=%fused_computation.2 | loop fusion | bytes 8388608 | tf_op jit(solution)/shard_map/slice | solution.py:577
  90.2 0.4 convert_bitcast_fusion.1
  90.6 5.2 %copy.11 = f32[512,4,2,256]{3,2,1,0:T(2,128)} copy(f32[512,4,2,256]{3,0,2,1:T(8,128)S(1)} %convert_bitcast_fusion.1) | data formatting | bytes 8388608 | tf_op jit(solution)/shard_map/convert_element_type | solution.py:578
  95.9 6.4 %reshape.37 = f32[512,2048]{1,0:T(8,128)} reshape(f32[512,4,2,256]{3,2,1,0:T(2,128)} %copy.11) | data formatting | bytes 8388608 | tf_op jit(solution)/shard_map/convert_element_type | solution.py:578
  102.3 0.4 convert_bitcast_fusion
  102.6 3.2 %copy.12 = f32[4,512,2,256]{3,2,1,0:T(2,128)S(1)} copy(f32[4,512,2,256]{3,1,2,0:T(8,128)S(1)} %convert_bitcast_fusion) | data formatting | bytes 8388608 | tf_op jit(solution)/shard_map/convert_element_type | solution.py:577
  105.9 0.0 copy-start
  105.9 2.5 %copy.13 = f32[256,8,2,256]{3,1,2,0:T(8,128)} copy(f32[256,8,2,256]{3,2,1,0:T(2,128)S(1)} %bitcast.15) | data formatting | bytes 8388608
  108.4 0.0 copy-done
  108.4 1.0 copy.15
Async XLA Ops:
  105.9 2.5 %copy-start = (bf16[1024,512]{1,0:T(8,128)(2,1)S(1)}, bf16[1024,512]{1,0:T(8,128)(2,1)}, u32[]{:S(2)}) copy-start(bf16[1024,512]{1,0:T(8,128)(2,1)} %get-tuple-element.8) | copy-start | bytes 3145732

commit v2 on v1

v2 whole, which is shorter than its diff:
```python
import jax
import jax.numpy as jnp
from jax import lax
from jax.experimental import pallas as pl
from jax.experimental.pallas import tpu as pltpu
from jax.sharding import PartitionSpec as P

EPS = 1e-06
ROWS, COLS, CH, FF = 8, 128, 512, 2048
PIX = ROWS * COLS
CHUNKS = (512, 512, 512, 256, 256)
STARTS = tuple(sum(CHUNKS[:n]) for n in range(len(CHUNKS)))
LEFT = 8
F32, BF16 = jnp.float32, jnp.bfloat16
MESH = pl.DeviceIdType.MESH
FIRST_AXIS = ((0, 2), (1, 0), (2, 1), (0, 2), (2, 0))
SIDES = ((-1, 0), (1, 0), (0, -1), (0, 1), (-1, -1), (-1, 1), (1, -1), (1, 1))
(R_CORE, R_A0, R_A1, R_B0, R_B1, R_PRS, R_PAG, R_G0, R_G1, R_H0, R_H1, R_CAG) = range(12)


def direct(c):
    return c > 1


def kernel(*refs):
    refs = list(refs)

    def take(n):
        out = refs[:n]
        del refs[:n]
        return out

    feat_hbm, dww_hbm, gain_hbm, wup_hbm, wdn_hbm, cot_hbm = take(6)
    gin_hbm, small_hbm = take(2)
    big_hbm = take(len(CHUNKS))
    fbuf, cbuf, wup, wdn, dww, gainb, xf, gp, wb, cv, nv, invb, sc = take(13)
    act, gh, gs, gb, obuf, scol, hrow, hcol, hcor = take(9)
    gd, dsm, dpr, dax, dga, dout = take(6)
    G, csend, crecv, M, axa, axs, axb, pls, plr, GA, GB = zip(*[take(11) for _ in CHUNKS])
    ld, hsend, hrecv, csem, rsem, ssend, srecv, osem = take(8)

    ra, ca = lax.axis_index("rows"), lax.axis_index("cols")
    core = ra % 2
    y, z, x = (ra // 2) % 4, ra // 8, ca

    def device(x_, y_, z_, core_):
        return ((z_ * 4 + y_) * 2 + core_, x_)

    partner = device(x, y, z, 1 - core)

    def side(dr, dc):
        return ((ra + dr + 32) % 32, (ca + dc + 4) % 4)

    def plane_peer(d, axis):
        ix, iy, iz = axis
        u, v = ix * y + iy * z + iz * x, ix * z + iy * x + iz * y
        u2, v2 = (u + d // 4) % 4, (v + d % 4) % 4
        return (
            device(
                ix * x + iy * v2 + iz * u2,
                ix * u2 + iy * y + iz * v2,
                ix * v2 + iy * u2 + iz * z,
                core,
            ),
            u2 * 4 + v2,
        )

    def plane_pos(axis):
        ix, iy, iz = axis
        return (ix * y + iy * z + iz * x) * 4 + ix * z + iy * x + iz * y

    def pair_peer(d):
        x2, y2, core2 = (x + d // 8) % 4, (y + (d // 2) % 4) % 4, (core + d % 2) % 2
        return device(x2, y2, z, core2), (x2 * 4 + y2) * 2 + core2

    def axis_of(c):
        a0, a1 = FIRST_AXIS[c]
        return tuple((a0 == n) * (1 - core) + (a1 == n) * core for n in range(3))

    def along(axis, step):
        ix, iy, iz = axis
        return device(
            (x + step * ix) % 4, (y + step * iy) % 4, (z + step * iz) % 4, core
        )

    def remote(src, dst, send, recv, to):
        return pltpu.make_async_remote_copy(
            src_ref=src, dst_ref=dst, send_sem=send, recv_sem=recv, device_id=to, device_id_type=MESH
        )

    def landed(ref, sem):
        pltpu.make_async_copy(ref, ref, sem).wait()

    loads = [
        pltpu.make_async_copy(s, d, ld.at[n])
        for n, (s, d) in enumerate(
            ((feat_hbm, fbuf), (dww_hbm, dww), (gain_hbm, gainb), (cot_hbm, cbuf), (wup_hbm, wup), (wdn_hbm, wdn))
        )
    ]
    for c_ in loads:
        c_.start()
    barrier = pltpu.get_barrier_semaphore()
    for dr, dc in SIDES:
        pl.semaphore_signal(barrier, inc=1, device_id=side(dr, dc), device_id_type=MESH)

    @pl.loop(1, 32)
    def _(d):
        pl.semaphore_signal(barrier, inc=1, device_id=pair_peer(d)[0], device_id_type=MESH)

    for axis in ((1, 0, 0), (0, 1, 0)):
        @pl.loop(1, 16)
        def _(d, axis=axis):
            pl.semaphore_signal(barrier, inc=1, device_id=plane_peer(d, axis)[0], device_id_type=MESH)

    for c_ in loads[:3]:
        c_.wait()

    def edges(pad, phase):
        for n, start in ((0, LEFT), (1, LEFT + COLS - 8)):
            for cc in range(4):
                scol[phase, n, :, :, cc * 128 : cc * 128 + 128] = pad[
                    cc, 3 : 3 + ROWS, start : start + 8, :
                ].astype(BF16)

    with jax.named_scope("widen"):
        @pl.loop(0, ROWS)
        def _(r):
            for cc in range(4):
                xf[cc, 3 + r, LEFT : LEFT + COLS, :] = fbuf[r, :, cc * 128 : cc * 128 + 128].astype(F32)

        edges(xf, 0)
        for cc in range(4):
            gd[cc, 48:64, :] = jnp.zeros((16, 128), F32)

    with jax.named_scope("entry"):
        pl.semaphore_wait(barrier, len(SIDES) + 31 + 30)

    def halo_copies(phase, rows_src):
        out = []
        for n, (dr, dc) in enumerate(SIDES):
            rs = slice(0, 3) if dr < 0 else slice(5, 8)
            if dc == 0:
                src, dst = rows_src.at[rs], hrow.at[phase, n]
            elif dr == 0:
                src, dst = scol.at[phase, n - 2], hcol.at[phase, n - 2]
            else:
                src, dst = scol.at[phase, 0 if dc < 0 else 1, rs], hcor.at[phase, n - 4]
            if dc == 0 and phase == 1:
                cols = [pl.ds(32 * k, 32) for k in range(4)]
                out.append([
                    remote(src.at[:, k], dst.at[:, k], hsend.at[1, n], hrecv.at[1, n], side(dr, dc)) for k in cols
                ])
            else:
                out.append([remote(src, dst, hsend.at[phase, n], hrecv.at[phase, n], side(dr, dc))])
        return out

    def halo_landed(phase, n):
        buf = hrow.at[phase, n] if n < 2 else hcol.at[phase, n - 2] if n < 4 else hcor.at[phase, n - 4]
        landed(buf, hrecv.at[phase, n])

    valid = {
        -1: jnp.where(ra < 31, 1.0, 0.0).astype(F32),
        1: jnp.where(ra > 0, 1.0, 0.0).astype(F32),
    }
    valid_c = {
        -1: jnp.where(ca < 3, 1.0, 0.0).astype(F32),
        1: jnp.where(ca > 0, 1.0, 0.0).astype(F32),
    }

    def halo_cols(phase, pad):
        for n in (2, 3):
            halo_landed(phase, n)
            dc = SIDES[n][1]
            start = LEFT + COLS if dc < 0 else LEFT - 8
            for cc in range(4):
                pad[cc, 3 : 3 + ROWS, start : start + 8, :] = (
                    hcol[phase, n - 2, :, :, cc * 128 : cc * 128 + 128].astype(F32) * valid_c[dc]
                )

    def halo_rows(phase, pad):
        for n in (0, 1):
            halo_landed(phase, n)
            dr = SIDES[n][0]
            r0 = 3 + ROWS if dr < 0 else 0
            for r in range(3):
                for cc in range(4):
                    pad[cc, r0 + r, LEFT : LEFT + COLS, :] = (
                        hrow[phase, n, r, :, cc * 128 : cc * 128 + 128].astype(F32) * valid[dr]
                    )
        for n in range(4, 8):
            halo_landed(phase, n)
            dr, dc = SIDES[n]
            r0 = 3 + ROWS if dr < 0 else 0
            start = LEFT + COLS if dc < 0 else LEFT - 8
            for cc in range(4):
                pad[cc, r0 : r0 + 3, start : start + 8, :] = hcor[
                    phase, n - 4, :, :, cc * 128 : cc * 128 + 128
                ].astype(F32) * (valid[dr] * valid_c[dc])

    def conv(pad, flip, cc, cb, inner):
        rhos = range(3, 11) if inner else (0, 1, 2, 11, 12, 13)
        rows = range(ROWS) if inner else (0, 1, 2, 5, 6, 7)
        base = cb * 32

        def at(r, b):
            return pl.ds(pl.multiple_of(r * COLS + base + 8 * b, 8), 8)

        def body(j, acc):
            acc = dict(zip([(r, b) for r in rows for b in range(4)], acc))
            w = [wb[cc, (48 - 7 * i - j) if flip else (7 * i + j)] for i in range(7)]
            for rho in rhos:
                for b in range(4):
                    v = pad[cc, rho, pl.ds(base + (8 * b + LEFT - 3) + j, 8), :]
                    for r in rows:
                        if 0 <= rho - r <= 6:
                            acc[r, b] = acc[r, b] + v * w[rho - r]
            return tuple(acc.values())

        if inner:
            start = tuple(jnp.zeros((8, 128), F32) for r in rows for b in range(4))
        else:
            start = tuple(cv[cc, at(r, b), :] for r in rows for b in range(4))
        acc = lax.fori_loop(0, 7, body, start, unroll=1 if inner else 7)
        for n, (r, b) in enumerate([(r, b) for r in rows for b in range(4)]):
            cv[cc, at(r, b), :] = acc[n]

    halo = halo_copies(0, fbuf)
    with jax.named_scope("taps"):
        for n in (2, 3, 0, 1, 4, 5, 6, 7):
            halo[n][0].start()

        for t in range(49):
            for cc in range(4):
                wb[cc, t] = jnp.broadcast_to(dww[t : t + 1, cc * 128 : cc * 128 + 128], (8, 128))

    with jax.named_scope("fconv_mid"):
        @pl.loop(0, 8)
        def _(t):
            conv(xf, False, t // 2, 1 + t % 2, True)

    with jax.named_scope("fhalo_c"):
        halo_cols(0, xf)

    with jax.named_scope("fconv_side"):
        @pl.loop(0, 8)
        def _(t):
            conv(xf, False, t // 2, 3 * (t % 2), True)

    with jax.named_scope("fhalo_r"):
        halo_rows(0, xf)

    with jax.named_scope("fconv_out"):
        @pl.loop(0, 16)
        def _(t):
            conv(xf, False, t // 4, t % 4, False)

    with jax.named_scope("norm"):
        def norm(t, carry):
            ps = pl.ds(pl.multiple_of(t * 64, 64), 64)
            v = [cv[cc, ps, :] for cc in range(4)]
            mean = jnp.sum(v[0] + v[1] + v[2] + v[3], axis=1, keepdims=True) * (1.0 / CH)
            v = [a - mean for a in v]
            sq = [a * a for a in v]
            inv = lax.rsqrt(jnp.sum(sq[0] + sq[1] + sq[2] + sq[3], axis=1, keepdims=True) * (1.0 / CH) + EPS)
            invb[ps, :] = jnp.broadcast_to(inv, (64, 128))
            for cc in range(4):
                n_ = v[cc] * inv
                nv[cc, ps, :] = n_
                sc[ps, cc * 128 : cc * 128 + 128] = (n_ * gainb[:, cc * 128 : cc * 128 + 128]).astype(BF16)
            return carry

        lax.fori_loop(0, 16, norm, 0, unroll=2)

    for c_ in loads[3:]:
        c_.wait()

    def mlp_a(c, half):
        w = CHUNKS[c]
        fs = slice(STARTS[c], STARTS[c] + w)
        for pb in (2 * half, 2 * half + 1):
            ps = slice(pb * 256, pb * 256 + 256)
            h = jnp.dot(sc[ps, :], wup[:, fs], preferred_element_type=F32)
            ga = lax.dot_general(cbuf[ps, :], wdn[fs, :], (((1,), (1,)), ((), ())), preferred_element_type=F32)
            phi = 0.5 * (1.0 + lax.erf(h * 0.7071067811865476))
            act[ps, 0:w] = (h * phi).astype(BF16)
            e = jnp.exp(-0.5 * h * h) * 0.3989422804014327
            gh[ps, fs] = (ga * (phi + h * e)).astype(BF16)

    def put(c, slot, value):
        w, rows = CHUNKS[c] // 2, value.shape[0]
        for n in range(1024 // rows):
            G[c][slot, n * rows : (n + 1) * rows, :] = value[:, n * w : (n + 1) * w]

    def mlp_down(c):
        put(c, core, lax.dot_general(
            act[:, 0 : CHUNKS[c]], cbuf[...], (((0,), (0,)), ((), ())), preferred_element_type=F32))

    def mlp_up(c):
        fs = slice(STARTS[c], STARTS[c] + CHUNKS[c])
        put(c, 1 - core, lax.dot_general(
            sc[...], gh[:, fs], (((0,), (0,)), ((), ())), preferred_element_type=F32))

    def mlp_back(q):
        ps = slice(q * 256, q * 256 + 256)
        gs[ps, :] = lax.dot_general(gh[ps, :], wup[...], (((1,), (1,)), ((), ())), preferred_element_type=F32)

    def blocks(fn):
        @pl.loop(0, 8)
        def _(t):
            fn(t // 2, pl.ds((t % 2) * 8, 8), pl.ds(pl.multiple_of(t * 128, 128), 128))

    def place(c):
        axis = axis_of(c)
        return axis, axis[0] * x + axis[1] * y + axis[2] * z

    def send(c, n, src, dst, to):
        remote(src, dst, csem.at[c, n], rsem.at[c, n], to).start()

    def arrived(c, n, ref):
        landed(ref, rsem.at[c, n])

    def ch_core(c):
        def go(a, n, rows):
            csend[c][a, n] = G[c][1, rows, :].reshape(8, 16, CHUNKS[c] // 2).astype(BF16)
        blocks(go)
        send(c, R_CORE, csend[c], crecv[c], partner)

    def ch_axis(c):
        arrived(c, R_CORE, crecv[c])
        axis, p = place(c)
        def go(a, n, rows):
            M[c][a, n] = (
                G[c][0, rows, :].reshape(8, 16, CHUNKS[c] // 2) + crecv[c][a, n].astype(F32)
            ).astype(BF16)
        blocks(go)
        if direct(c):
            for d in (2, 1, 3):
                send(c, R_A0, M[c].at[(p + d) % 4], axb[c].at[d - 1], along(axis, d))
        else:
            far = (p + 2) % 4
            send(c, R_A0, M[c].at[far, 0:8], axa[c].at[0], along(axis, 1))
            send(c, R_A1, M[c].at[far, 8:16], axa[c].at[1], along(axis, 3))

    def ch_axis2(c):
        axis, p = place(c)
        arrived(c, R_A0, axa[c].at[0])
        arrived(c, R_A1, axa[c].at[1])
        right, left = (p + 1) % 4, (p + 3) % 4
        axs[c][0, 0:8] = (M[c][right, 0:8].astype(F32) + axa[c][0].astype(F32)).astype(BF16)
        axs[c][0, 8:16] = M[c][right, 8:16]
        send(c, R_B0, axs[c].at[0], axb[c].at[0], along(axis, 1))
        axs[c][1, 0:8] = M[c][left, 0:8]
        axs[c][1, 8:16] = (M[c][left, 8:16].astype(F32) + axa[c][1].astype(F32)).astype(BF16)
        send(c, R_B1, axs[c].at[1], axb[c].at[1], along(axis, 3))

    def ch_plane(c):
        axis, p = place(c)
        if direct(c):
            arrived(c, R_A0, axb[c])
        else:
            arrived(c, R_B0, axb[c].at[0])
            arrived(c, R_B1, axb[c].at[1])
        total = M[c][p].astype(F32)
        for n in range(3 if direct(c) else 2):
            total = total + axb[c][n].astype(F32)
        pls[c][...] = total.astype(BF16)

        @pl.loop(1, 16, unroll=5)
        def _(d):
            to, pos = plane_peer(d, axis)
            send(c, R_PRS, pls[c].at[pos], plr[c].at[d - 1], to)

    def ch_share(c):
        axis, p = place(c)
        pos = plane_pos(axis)
        arrived(c, R_PRS, plr[c])
        total = pls[c][pos].astype(F32)
        for d in range(15):
            total = total + plr[c][d].astype(F32)
        GA[c][p, pos] = total.astype(BF16)

        @pl.loop(1, 16, unroll=5)
        def _(d):
            to, _ = plane_peer(d, axis)
            send(c, R_PAG, GA[c].at[p, pos], GA[c].at[p, pos], to)

    def ch_back(c):
        axis, p = place(c)
        arrived(c, R_PAG, plr[c])
        if direct(c):
            for d in (2, 1, 3):
                send(c, R_G0, GA[c].at[p], GA[c].at[p], along(axis, d))
        else:
            send(c, R_G0, GA[c].at[p], GA[c].at[p], along(axis, 1))
            send(c, R_G1, GA[c].at[p], GA[c].at[p], along(axis, 3))
        send(c, R_CAG, GA[c].at[p], GB[c].at[p], partner)

    def ch_back2(c):
        axis, p = place(c)
        right, left = (p + 1) % 4, (p + 3) % 4
        arrived(c, R_G0, GA[c].at[left])
        arrived(c, R_G1, GA[c].at[right])
        a, b = GA[c].at[left, 0:8], GA[c].at[right, 8:16]
        send(c, R_H0, a, a, along(axis, 1))
        send(c, R_H1, b, b, along(axis, 3))
        for q in (left, right):
            send(c, R_CAG, GA[c].at[q], GB[c].at[q], partner)

    def ch_pair(c):
        axis, p = place(c)
        if direct(c):
            arrived(c, R_G0, axb[c])
            for d in (1, 2, 3):
                q = (p + d) % 4
                send(c, R_CAG, GA[c].at[q], GB[c].at[q], partner)
        else:
            arrived(c, R_H0, axa[c].at[0])
            arrived(c, R_H1, axa[c].at[1])
            far = (p + 2) % 4
            send(c, R_CAG, GA[c].at[far], GB[c].at[far], partner)
        pltpu.make_async_copy(GA[c], big_hbm[c].at[core], osem.at[2 * c]).start()

    def ch_end(c):
        arrived(c, R_CAG, GB[c])
        pltpu.make_async_copy(GB[c], big_hbm[c].at[1 - core], osem.at[2 * c + 1]).start()

    def ln_back(quarter):
        def body(t, part):
            ps = slice(quarter * 256 + t * 64, quarter * 256 + t * 64 + 64)
            inv = invb[ps, :]
            ns = [nv[cc, ps, :] for cc in range(4)]
            gv = [gs[ps, cc * 128 : cc * 128 + 128] for cc in range(4)]
            prod = [g * n for g, n in zip(gv, ns)]
            part = tuple(
                q + jnp.sum(pr.reshape(8, 8, 128), axis=0) for q, pr in zip(part, prod)
            )
            gains = [gainb[:, cc * 128 : cc * 128 + 128] for cc in range(4)]
            gn = [g * k for g, k in zip(gv, gains)]
            gm = [pr * k for pr, k in zip(prod, gains)]
            m1 = jnp.sum(gn[0] + gn[1] + gn[2] + gn[3], axis=1, keepdims=True) * (1.0 / CH)
            m2 = jnp.sum(gm[0] + gm[1] + gm[2] + gm[3], axis=1, keepdims=True) * (1.0 / CH)
            r, c0 = 2 * quarter + t // 2, (t % 2) * 64
            for cc in range(4):
                g = (inv * (gn[cc] - m1 - ns[cc] * m2)).astype(BF16)
                gb[r, c0 : c0 + 64, cc * 128 : cc * 128 + 128] = g
                gp[cc, 3 + r, LEFT + c0 : LEFT + c0 + 64, :] = g.astype(F32)
            return part

        part = tuple(jnp.zeros((8, 128), F32) for _ in range(4))
        for t in range(4):
            part = body(t, part)
        for cc in range(4):
            row = jnp.sum(part[cc], axis=0, keepdims=True)
            gd[cc, 49:50, :] = row if quarter == 0 else gd[cc, 49:50, :] + row

    back = halo_copies(1, gb)

    def send_back():
        edges(gp, 1)
        for n in (2, 3, 4, 5, 6, 7):
            back[n][0].start()

    def send_rows(k):
        back[0][k].start()
        back[1][k].start()

    def gdw(cc, js):
        @pl.loop(js[0], js[1])
        def _(j):
            def body(cb, acc):
                acc = list(acc)
                base = cb * 64
                for b in range(8):
                    gv = [gp[cc, 3 + r, pl.ds(pl.multiple_of(base + LEFT + 8 * b, 8), 8), :] for r in range(8)]
                    for rho in range(14):
                        v = xf[cc, rho, pl.ds(base + (8 * b + LEFT - 3) + j, 8), :]
                        for r in range(max(0, rho - 6), min(8, rho + 1)):
                            acc[rho - r] = acc[rho - r] + v * gv[r]
                return tuple(acc)

            acc = lax.fori_loop(0, 2, body, tuple(jnp.zeros((8, 128), F32) for _ in range(7)))
            for i in range(7):
                gd[cc, pl.ds(7 * i + j, 1), :] = jnp.sum(acc[i], axis=0, keepdims=True)

    zaxis = (0, 0, 1)
    mine = (x * 4 + y) * 2 + core
    OUT = 2 * len(CHUNKS)

    def sm_scatter():
        for cc in range(4):
            for tb in range(8):
                dsm[8 * cc + tb] = gd[cc, 8 * tb : 8 * tb + 8, :]

        @pl.loop(1, 32)
        def _(d):
            to, pos = pair_peer(d)
            remote(dsm.at[pos], dpr.at[d - 1], ssend.at[0], srecv.at[0], to).start()

    def sm_axis():
        landed(dpr, srecv.at[0])
        total = dsm[mine]
        for d in range(31):
            total = total + dpr[d]
        dax[z] = total
        for step in (2, 1, 3):
            remote(dax.at[z], dax.at[z], ssend.at[1], srecv.at[1], along(zaxis, step)).start()

    def sm_share():
        landed(dpr.at[0:3], srecv.at[1])
        dga[mine] = dax[0] + dax[1] + dax[2] + dax[3]

        @pl.loop(1, 32)
        def _(d):
            to, _ = pair_peer(d)
            remote(dga.at[mine], dga.at[mine], ssend.at[2], srecv.at[2], to).start()

    def sm_end():
        landed(dpr, srecv.at[2])
        for cc in range(4):
            for tb in range(8):
                dout[8 * tb : 8 * tb + 8, cc * 128 : cc * 128 + 128] = dga[8 * cc + tb]
        pltpu.make_async_copy(dout, small_hbm, osem.at[OUT]).start()

    def gin_inner(cb, half):
        @pl.loop(2 * half, 2 * half + 2)
        def _(t):
            conv(gp, True, t, cb, True)

    def gin_outer(cb):
        @pl.loop(0, 4)
        def _(t):
            conv(gp, True, t, cb, False)

    def gin_store(part):
        @pl.loop(part * 8, part * 8 + 8)
        def _(t):
            ps = pl.ds(pl.multiple_of(t * 64, 64), 64)
            for cc in range(4):
                cs = slice(cc * 128, cc * 128 + 128)
                obuf[ps, cs] = (cbuf[ps, cs].astype(F32) + cv[cc, ps, :]).astype(BF16)
        rows = slice(part * 512, part * 512 + 512)
        pltpu.make_async_copy(obuf.at[rows], gin_hbm.at[rows], osem.at[OUT + 1 + part]).start()

    work = []
    chains = {}
    for c, w in enumerate(CHUNKS):
        k = w / 512
        work += [(0.75 * k, "mlp_a", lambda c=c: mlp_a(c, 0), None), (0.75 * k, "mlp_a", lambda c=c: mlp_a(c, 1), None)]
        work += [(0.73 * k, "mlp_down", lambda c=c: mlp_down(c), None), (0.73 * k, "mlp_up", lambda c=c: mlp_up(c), c)]
        if direct(c):
            steps = (
                (0.0, ch_core), (2.2, ch_axis), (5.5, ch_plane), (7.0, ch_share), (6.0, ch_back), (6.0, ch_pair), (2.5, ch_end)
            )
        else:
            steps = (
                (0.0, ch_core), (2.5, ch_axis), (4.0, ch_axis2), (5.0, ch_plane), (7.0, ch_share),
                (6.0, ch_back), (5.0, ch_back2), (5.0, ch_pair), (2.5, ch_end),
            )
        chains[c] = [(gap, fn.__name__, lambda fn=fn, c=c: fn(c)) for gap, fn in steps]
    def both(q):
        if q < 4:
            mlp_back(q)
        if q > 0:
            ln_back(q - 1)

    work += [(0.73, "back", lambda q=q: both(q), None) for q in range(5)]
    work += [(0.1, "send_back", send_back, None)]
    small = len(CHUNKS)
    for cc in range(4):
        work += [(0.8, "gdw", lambda cc=cc: gdw(cc, (0, 3)), None)]
        work += [(0.02, "send_rows", lambda cc=cc: send_rows(cc), None)]
        work += [(0.55, "gdw", lambda cc=cc: gdw(cc, (3, 5)), None)]
        work += [(0.55, "gdw", lambda cc=cc: gdw(cc, (5, 7)), small if cc == 3 else None)]
    steps = ((0.0, sm_scatter), (4.6, sm_axis), (3.6, sm_share), (6.0, sm_end))
    chains[small] = [(gap, fn.__name__, fn) for gap, fn in steps]
    for n, cb in enumerate((1, 2, 0, 3)):
        if n == 2:
            work += [(0.05, "halo_c", lambda: halo_cols(1, gp), None)]
        work += [(0.85, "gin_in", lambda cb=cb, half=half: gin_inner(cb, half), None) for half in (0, 1)]
    work += [(0.15, "halo_r", lambda: halo_rows(1, gp), None)]
    work += [(0.7, "gin_out", lambda cb=cb: gin_outer(cb), None) for cb in range(4)]
    work += [(0.2, "gin_st", lambda: gin_store(0), None), (0.2, "gin_st", lambda: gin_store(1), None)]

    now = 0.0
    due = []

    def serve(limit):
        nonlocal now
        while due and (limit is None or min(due)[0] <= limit):
            when, key, n = min(due)
            due.remove((when, key, n))
            now = max(now, when) + 0.1
            with jax.named_scope(f"{chains[key][n][1]}_{key}"):
                chains[key][n][2]()
            if n + 1 < len(chains[key]):
                due.append((now + chains[key][n + 1][0], key, n + 1))

    for cost, name, fn, opens in work:
        with jax.named_scope(name):
            fn()
        now += cost
        if opens is not None:
            due.append((now, opens, 0))
        serve(now)
    serve(None)

    with jax.named_scope("drain"):
        for phase in (0, 1):
            for n in range(8):
                buf = hrow.at[phase, n] if n < 2 else hcol.at[phase, n - 2] if n < 4 else hcor.at[phase, n - 4]
                landed(buf, hsend.at[phase, n])
        for c in range(len(CHUNKS)):
            sent = [(R_CORE, csend[c]), (R_PRS, plr[c]), (R_PAG, plr[c]), (R_CAG, GA[c])]
            if direct(c):
                sent += [(R_A0, axb[c]), (R_G0, axb[c])]
            else:
                sent += [(R_A0, axa[c].at[0]), (R_A1, axa[c].at[1]), (R_B0, axb[c].at[0]), (R_B1, axb[c].at[1])]
                sent += [(R_G0, axb[c].at[0]), (R_G1, axb[c].at[1]), (R_H0, axa[c].at[0]), (R_H1, axa[c].at[1])]
            for n, ref in sent:
                landed(ref, csem.at[c, n])
            pltpu.make_async_copy(GA[c], big_hbm[c].at[core], osem.at[2 * c]).wait()
            pltpu.make_async_copy(GB[c], big_hbm[c].at[1 - core], osem.at[2 * c + 1]).wait()
        landed(dpr, ssend.at[0])
        landed(dpr.at[0:3], ssend.at[1])
        landed(dpr, ssend.at[2])
        pltpu.make_async_copy(dout, small_hbm, osem.at[OUT]).wait()
        for part in (0, 1):
            rows = slice(part * 512, part * 512 + 512)
            pltpu.make_async_copy(obuf.at[rows], gin_hbm.at[rows], osem.at[OUT + 1 + part]).wait()


def finish_kernel(*refs):
    refs = list(refs)
    n_ch = len(CHUNKS)
    gin_hbm, small_hbm = refs[:2]
    big_hbm = refs[2 : 2 + n_ch]
    gout_hbm, dw_hbm, gain_hbm, up_hbm, down_hbm, gbuf, sbuf, dbuf, kbuf = refs[2 + n_ch : 11 + n_ch]
    narrow = refs[11 + n_ch : 11 + 2 * n_ch]
    downs = refs[11 + 2 * n_ch : 11 + 3 * n_ch]
    ups = refs[11 + 3 * n_ch : 11 + 4 * n_ch]
    isem, osem = refs[11 + 4 * n_ch :]
    ins = [
        [pltpu.make_async_copy(big_hbm[c].at[s], narrow[c].at[s], isem.at[2 * c + s]) for s in range(2)]
        for c in range(n_ch)
    ]
    for pair in ins:
        for c_ in pair:
            c_.start()
    first = pltpu.make_async_copy(gin_hbm, gbuf, isem.at[2 * n_ch])
    second = pltpu.make_async_copy(small_hbm, sbuf, isem.at[2 * n_ch + 1])
    first.start()
    second.start()
    outs = []

    def put(src, dst):
        outs.append(pltpu.make_async_copy(src, dst, osem.at[len(outs)]))
        outs[-1].start()

    for c, w in enumerate(CHUNKS):
        half = w // 2
        for s in range(2):
            ins[c][s].wait()
            wide = (downs, ups)[s][c]
            rows = wide.shape[0]
            step = min(rows, 1024) // 4

            @pl.loop(0, 4)
            def _(t):
                rs = pl.ds(pl.multiple_of(t * step, step), step)
                for n in range(1024 // rows):
                    wide[rs, n * half : (n + 1) * half] = narrow[c][
                        s, pl.ds(pl.multiple_of(n * rows + t * step, step), step), :
                    ].astype(F32)

            part = pl.ds(STARTS[c], w)
            put(wide, down_hbm.at[part] if s == 0 else up_hbm.at[:, part])
    first.wait()
    put(gbuf, gout_hbm)
    second.wait()
    dbuf[...] = sbuf[0:49, :]
    kbuf[...] = sbuf[49:50, :]
    put(dbuf, dw_hbm)
    put(kbuf, gain_hbm)
    for c_ in outs:
        c_.wait()


def finish(gin, small, big):
    vm, dma = pltpu.VMEM, pltpu.SemaphoreType.DMA
    any_ = pl.BlockSpec(memory_space=pl.ANY)
    n_ch = len(CHUNKS)
    gin, dw, gain, up, down = pl.pallas_call(
        finish_kernel,
        out_shape=(
            jax.ShapeDtypeStruct((PIX, CH), BF16),
            jax.ShapeDtypeStruct((49, CH), F32),
            jax.ShapeDtypeStruct((1, CH), F32),
            jax.ShapeDtypeStruct((CH, FF), F32),
            jax.ShapeDtypeStruct((FF, CH), F32),
        ),
        in_specs=[any_] * (2 + n_ch),
        out_specs=[any_] * 5,
        scratch_shapes=[vm((PIX, CH), BF16), vm((64, CH), F32), vm((49, CH), F32), vm((1, CH), F32)]
        + [vm((2, 1024, w // 2), BF16) for w in CHUNKS]
        + [vm((w, CH), F32) for w in CHUNKS]
        + [vm((CH, w), F32) for w in CHUNKS]
        + [dma((2 * n_ch + 2,)), dma((2 * n_ch + 3,))],
        compiler_params=pltpu.CompilerParams(vmem_limit_bytes=66_000_000),
        name="finish",
    )(gin, small, *[b.reshape(2, 1024, w // 2) for b, w in zip(big, CHUNKS)])
    return gin.reshape(ROWS, COLS, CH), dw, gain.reshape(CH), up, down


def on_device(features, dw_weight, norm_gain, w_up, w_down, cotangent):
    vm, dma = pltpu.VMEM, pltpu.SemaphoreType.DMA
    any_ = pl.BlockSpec(memory_space=pl.ANY)
    n_ch = len(CHUNKS)
    comm = []
    for c, w in enumerate(CHUNKS):
        h = w // 2
        whole = vm((4, 16, 16, h), BF16)
        comm += [vm((2, 1024, h), F32), whole, whole, whole]
        comm += [vm((2, 8, 16, h), BF16), vm((2, 16, 16, h), BF16), vm((3 if direct(c) else 2, 16, 16, h), BF16)]
        comm += [vm((16, 16, h), BF16), vm((15, 16, h), BF16), whole, whole]
    gin, small, *big = pl.pallas_call(
        kernel,
        out_shape=(
            jax.ShapeDtypeStruct((PIX, CH), BF16),
            jax.ShapeDtypeStruct((64, CH), F32),
            *[jax.ShapeDtypeStruct((2, 4, 16, 16, w // 2), BF16) for w in CHUNKS],
        ),
        in_specs=[any_] * 6,
        out_specs=[any_] * (2 + n_ch),
        scratch_shapes=[
            vm((ROWS, COLS, CH), BF16), vm((PIX, CH), BF16), vm((CH, FF), BF16), vm((FF, CH), BF16),
            vm((49, CH), F32), vm((1, CH), F32),
            vm((4, 14, 144, 128), F32), vm((4, 14, 144, 128), F32), vm((4, 49, 8, 128), F32),
            vm((4, PIX, 128), F32), vm((4, PIX, 128), F32), vm((PIX, 128), F32), vm((PIX, CH), BF16),
            vm((PIX, max(CHUNKS)), BF16), vm((PIX, FF), BF16), vm((PIX, CH), F32),
            vm((ROWS, COLS, CH), BF16), vm((PIX, CH), BF16),
            vm((2, 2, 8, 8, CH), BF16), vm((2, 2, 3, COLS, CH), BF16), vm((2, 2, 8, 8, CH), BF16), vm((2, 4, 3, 8, CH), BF16),
            vm((4, 64, 128), F32), vm((32, 8, 128), F32), vm((31, 8, 128), F32), vm((4, 8, 128), F32),
            vm((32, 8, 128), F32), vm((64, CH), F32),
        ]
        + comm
        + [
            dma((6,)), dma((2, 8)), dma((2, 8)), dma((n_ch, 12)), dma((n_ch, 12)), dma((3,)), dma((3,)), dma((2 * n_ch + 3,)),
        ],
        compiler_params=pltpu.CompilerParams(
            collective_id=0, has_side_effects=True, vmem_limit_bytes=67_000_000
        ),
        name="block_backward",
    )(features, dw_weight, norm_gain.reshape(1, CH), w_up, w_down, cotangent.reshape(PIX, CH))
    return finish(gin, small, big)


def solution(mesh):
    return jax.shard_map(
        on_device,
        mesh=mesh,
        in_specs=(P("rows", "cols", None), P(), P(), P(), P(), P("rows", "cols", None)),
        out_specs=(P("rows", "cols", None), P(), P(), P(), P()),
        check_vma=False,
    )
```

time: 110 us -> 77.7 us (0.71)
  local copies, waits for them, and re-layouts: 23.7 us -> 0 us
  Pallas kernels: 84.2 us -> 76.8 us
    convert_element_type x3 -> x0, local copies, waits for them, and re-layouts: 14.9 us -> none  [the longest x2 11.7 us: on_device(): grad_up = big[1].transpose(2, 0, 1, 3).reshape(CH, FF).astype(F32)]
    pallas_call x1, Pallas kernels: 84.2 us -> 71.8 us  [on_device(): pl.pallas_call(kernel, out_shape=(jax.ShapeDtypeStruct((PIX, CH), BF16),...]
    slice x3 -> x0, local copies, waits for them, and re-layouts: 5.37 us -> none  [the longest x1 2.52 us: on_device(): grad_down = big[0].transpose(0, 2, 1, 3).reshape(FF, CH).astype(F32)]
    pallas_call x0 -> x1, Pallas kernels: none -> 4.95 us  [finish(): pl.pallas_call(finish_kernel, out_shape=(jax.ShapeDtypeStruct((PIX, CH),...]
    unnamed x4 -> x0, local copies, waits for them, and re-layouts: 3.43 us -> none
where the time goes in v2:
time: 77.7 us; the launch traced here: 77.6 us
  Pallas kernels  76.8 us (99%)
  between operations  0.8 us (1%)
    pallas_call x1, Pallas kernels, on_device(): pl.pallas_call(kernel, out_shape=(jax.ShapeDtypeStruct((PIX, CH), BF16),...  71.8 us
    pallas_call x1, Pallas kernels, finish(): pl.pallas_call(finish_kernel, out_shape=(jax.ShapeDtypeStruct((PIX, CH),...  4.95 us

profile of v2, /device:TPU:1, one launch (start us, length us, event | category | flops | bytes accessed | tf_op | source)
XLA Modules:
  0.0 77.6 jit_solution(6910255571008421930)
XLA Ops:
  0.6 71.8 %block_backward.1 = (bf16[1024,512]{1,0:T(8,128)(2,1)}, f32[64,512]{1,0:T(8,128)}, bf16[2,4,16,16,256]{4,3,2,1,0:T(8,128)(2,1)}, bf16[2,4,16,16,256]{4,3,2,1,0:T...) custom-call(bf16[8,128,512]{2,1,0:T(8,128)(2,1)} %refs_0_.1, ...), custom_call_target="tpu_custom_call" | custom-call | tf_op jit(solution)/shard_map/block_backward/pallas_call | solution.py:725
  72.5 5.0 %finish.1 = (bf16[1024,512]{1,0:T(8,128)(2,1)}, f32[49,512]{1,0:T(8,128)}, f32[1,512]{1,0:T(1,128)}, f32[512,2048]{1,0:T(8,128)}, f32[2048,512]{1,0:T(8,128)}) custom-call(bf16[1024,512]{1,0:T(8,128)(2,1)} %get-tuple-element.17.refs_0_, f32[64,512]{1,0:T(8,128)} %get-tuple-element.18.refs_1_, bf16[2,1024,256]{2,1,0:T(8,128)(2,1)} %bitcast.10, ...), custom_call_target="tpu_custom_call" | custom-call | tf_op jit(solution)/shard_map/finish/pallas_call | solution.py:692

commit v3 on v2

--- a/solution.py
+++ b/solution.py
@@ -31,13 +31,13 @@
         return out
 
     feat_hbm, dww_hbm, gain_hbm, wup_hbm, wdn_hbm, cot_hbm = take(6)
-    gin_hbm, small_hbm = take(2)
-    big_hbm = take(len(CHUNKS))
+    obuf, dout = take(2)
+    GA, GB = take(len(CHUNKS)), take(len(CHUNKS))
     fbuf, cbuf, wup, wdn, dww, gainb, xf, gp, wb, cv, nv, invb, sc = take(13)
-    act, gh, gs, gb, obuf, scol, hrow, hcol, hcor = take(9)
-    gd, dsm, dpr, dax, dga, dout = take(6)
-    G, csend, crecv, M, axa, axs, axb, pls, plr, GA, GB = zip(*[take(11) for _ in CHUNKS])
-    ld, hsend, hrecv, csem, rsem, ssend, srecv, osem = take(8)
+    act, gh, gs, gb, scol, hrow, hcol, hcor = take(8)
+    gd, dsm, dpr, dax, dga = take(5)
+    G, csend, crecv, M, axa, axs, axb, pls, plr = zip(*[take(9) for _ in CHUNKS])
+    ld, hsend, hrecv, csem, rsem, ssend, srecv, near = take(8)
 
     ra, ca = lax.axis_index("rows"), lax.axis_index("cols")
     core = ra % 2
@@ -103,14 +103,16 @@
     for dr, dc in SIDES:
         pl.semaphore_signal(barrier, inc=1, device_id=side(dr, dc), device_id_type=MESH)
 
-    @pl.loop(1, 32)
-    def _(d):
-        pl.semaphore_signal(barrier, inc=1, device_id=pair_peer(d)[0], device_id_type=MESH)
-
-    for axis in ((1, 0, 0), (0, 1, 0)):
-        @pl.loop(1, 16)
-        def _(d, axis=axis):
-            pl.semaphore_signal(barrier, inc=1, device_id=plane_peer(d, axis)[0], device_id_type=MESH)
+    NEAR = [along(tuple(int(n == k) for n in range(3)), step) for k in range(3) for step in (1, 3)]
+    for to in NEAR:
+        pl.semaphore_signal(barrier, inc=1, device_id=to, device_id_type=MESH)
+
+    def round_signal(n):
+        for to in [partner] + NEAR:
+            pl.semaphore_signal(near.at[n], inc=1, device_id=to, device_id_type=MESH)
+
+    def round_wait(n):
+        pl.semaphore_wait(near.at[n], 1 + len(NEAR))
 
     for c_ in loads[:3]:
         c_.wait()
@@ -133,7 +135,8 @@
             gd[cc, 48:64, :] = jnp.zeros((16, 128), F32)
 
     with jax.named_scope("entry"):
-        pl.semaphore_wait(barrier, len(SIDES) + 31 + 30)
+        pl.semaphore_wait(barrier, len(SIDES) + len(NEAR))
+        round_signal(0)
 
     def halo_copies(phase, rows_src):
         out = []
@@ -220,7 +223,7 @@
             start = tuple(jnp.zeros((8, 128), F32) for r in rows for b in range(4))
         else:
             start = tuple(cv[cc, at(r, b), :] for r in rows for b in range(4))
-        acc = lax.fori_loop(0, 7, body, start, unroll=1 if inner else 7)
+        acc = lax.fori_loop(0, 7, body, start, unroll=7)
         for n, (r, b) in enumerate([(r, b) for r in rows for b in range(4)]):
             cv[cc, at(r, b), :] = acc[n]
 
@@ -239,6 +242,8 @@
             conv(xf, False, t // 2, 1 + t % 2, True)
 
     with jax.named_scope("fhalo_c"):
+        round_wait(0)
+        round_signal(1)
         halo_cols(0, xf)
 
     with jax.named_scope("fconv_side"):
@@ -247,6 +252,8 @@
             conv(xf, False, t // 2, 3 * (t % 2), True)
 
     with jax.named_scope("fhalo_r"):
+        round_wait(1)
+        round_signal(2)
         halo_rows(0, xf)
 
     with jax.named_scope("fconv_out"):
@@ -254,9 +261,12 @@
         def _(t):
             conv(xf, False, t // 4, t % 4, False)
 
-    with jax.named_scope("norm"):
-        def norm(t, carry):
-            ps = pl.ds(pl.multiple_of(t * 64, 64), 64)
+    round_wait(2)
+    round_signal(3)
+
+    def norm(quarter):
+        for t in range(4):
+            ps = slice(quarter * 256 + t * 64, quarter * 256 + t * 64 + 64)
             v = [cv[cc, ps, :] for cc in range(4)]
             mean = jnp.sum(v[0] + v[1] + v[2] + v[3], axis=1, keepdims=True) * (1.0 / CH)
             v = [a - mean for a in v]
@@ -267,17 +277,17 @@
                 n_ = v[cc] * inv
                 nv[cc, ps, :] = n_
                 sc[ps, cc * 128 : cc * 128 + 128] = (n_ * gainb[:, cc * 128 : cc * 128 + 128]).astype(BF16)
-            return carry
-
-        lax.fori_loop(0, 16, norm, 0, unroll=2)
 
     for c_ in loads[3:]:
         c_.wait()
 
-    def mlp_a(c, half):
+    def last_round():
+        round_wait(3)
+
+    def mlp_a(c, pbs):
         w = CHUNKS[c]
         fs = slice(STARTS[c], STARTS[c] + w)
-        for pb in (2 * half, 2 * half + 1):
+        for pb in pbs:
             ps = slice(pb * 256, pb * 256 + 256)
             h = jnp.dot(sc[ps, :], wup[:, fs], preferred_element_type=F32)
             ga = lax.dot_general(cbuf[ps, :], wdn[fs, :], (((1,), (1,)), ((), ())), preferred_element_type=F32)
@@ -418,11 +428,9 @@
             arrived(c, R_H1, axa[c].at[1])
             far = (p + 2) % 4
             send(c, R_CAG, GA[c].at[far], GB[c].at[far], partner)
-        pltpu.make_async_copy(GA[c], big_hbm[c].at[core], osem.at[2 * c]).start()
 
     def ch_end(c):
         arrived(c, R_CAG, GB[c])
-        pltpu.make_async_copy(GB[c], big_hbm[c].at[1 - core], osem.at[2 * c + 1]).start()
 
     def ln_back(quarter):
         def body(t, part):
@@ -484,7 +492,6 @@
 
     zaxis = (0, 0, 1)
     mine = (x * 4 + y) * 2 + core
-    OUT = 2 * len(CHUNKS)
 
     def sm_scatter():
         for cc in range(4):
@@ -519,7 +526,6 @@
         for cc in range(4):
             for tb in range(8):
                 dout[8 * tb : 8 * tb + 8, cc * 128 : cc * 128 + 128] = dga[8 * cc + tb]
-        pltpu.make_async_copy(dout, small_hbm, osem.at[OUT]).start()
 
     def gin_inner(cb, half):
         @pl.loop(2 * half, 2 * half + 2)
@@ -538,25 +544,35 @@
             for cc in range(4):
                 cs = slice(cc * 128, cc * 128 + 128)
                 obuf[ps, cs] = (cbuf[ps, cs].astype(F32) + cv[cc, ps, :]).astype(BF16)
-        rows = slice(part * 512, part * 512 + 512)
-        pltpu.make_async_copy(obuf.at[rows], gin_hbm.at[rows], osem.at[OUT + 1 + part]).start()
+
+    def norm_a():
+        for q in range(5):
+            if q < 4:
+                norm(q)
+            if q > 0:
+                mlp_a(0, (q - 1,))
 
     work = []
     chains = {}
     for c, w in enumerate(CHUNKS):
         k = w / 512
-        work += [(0.75 * k, "mlp_a", lambda c=c: mlp_a(c, 0), None), (0.75 * k, "mlp_a", lambda c=c: mlp_a(c, 1), None)]
+        if c == 0:
+            work += [(3.0, "norm_a", norm_a, None)]
+        else:
+            work += [(0.75 * k, "mlp_a", lambda c=c, p=p: mlp_a(c, p), None) for p in ((0, 1), (2, 3))]
+        if c == 1:
+            work += [(0.01, "last_round", last_round, None)]
         work += [(0.73 * k, "mlp_down", lambda c=c: mlp_down(c), None), (0.73 * k, "mlp_up", lambda c=c: mlp_up(c), c)]
         if direct(c):
             steps = (
-                (0.0, ch_core), (2.2, ch_axis), (5.5, ch_plane), (7.0, ch_share), (6.0, ch_back), (6.0, ch_pair), (2.5, ch_end)
+                (0.0, ch_core), (2.2, ch_axis), (5.0 + 2.0 * k, ch_plane), (7.0, ch_share), (6.0, ch_back), (6.0, ch_pair), (2.5, ch_end)
             )
         else:
             steps = (
                 (0.0, ch_core), (2.5, ch_axis), (4.0, ch_axis2), (5.0, ch_plane), (7.0, ch_share),
                 (6.0, ch_back), (5.0, ch_back2), (5.0, ch_pair), (2.5, ch_end),
             )
-        chains[c] = [(gap, fn.__name__, lambda fn=fn, c=c: fn(c)) for gap, fn in steps]
+        chains[c] = [((0.85 if n < 4 else 0.85) * gap, fn.__name__, lambda fn=fn, c=c: fn(c)) for n, (gap, fn) in enumerate(steps)]
     def both(q):
         if q < 4:
             mlp_back(q)
@@ -595,6 +611,27 @@
             if n + 1 < len(chains[key]):
                 due.append((now + chains[key][n + 1][0], key, n + 1))
 
+    def drain(chunks, steps):
+        for c in chunks:
+            sent = [(R_CORE, csend[c]), (R_PRS, plr[c]), (R_PAG, plr[c]), (R_CAG, GA[c])]
+            if direct(c):
+                sent += [(R_A0, axb[c]), (R_G0, axb[c])]
+            else:
+                sent += [(R_A0, axa[c].at[0]), (R_A1, axa[c].at[1]), (R_B0, axb[c].at[0]), (R_B1, axb[c].at[1])]
+                sent += [(R_G0, axb[c].at[0]), (R_G1, axb[c].at[1]), (R_H0, axa[c].at[0]), (R_H1, axa[c].at[1])]
+            for n, ref in sent:
+                if n in steps:
+                    landed(ref, csem.at[c, n])
+
+    def early_drain():
+        for phase in (0, 1):
+            for n in range(8):
+                buf = hrow.at[phase, n] if n < 2 else hcol.at[phase, n - 2] if n < 4 else hcor.at[phase, n - 4]
+                landed(buf, hsend.at[phase, n])
+        drain(range(len(CHUNKS)), (R_CORE, R_A0, R_A1, R_B0, R_B1, R_PRS, R_PAG))
+        landed(dpr, ssend.at[0])
+        landed(dpr.at[0:3], ssend.at[1])
+
     for cost, name, fn, opens in work:
         with jax.named_scope(name):
             fn()
@@ -602,83 +639,59 @@
         if opens is not None:
             due.append((now, opens, 0))
         serve(now)
+    with jax.named_scope("early"):
+        early_drain()
     serve(None)
 
     with jax.named_scope("drain"):
-        for phase in (0, 1):
-            for n in range(8):
-                buf = hrow.at[phase, n] if n < 2 else hcol.at[phase, n - 2] if n < 4 else hcor.at[phase, n - 4]
-                landed(buf, hsend.at[phase, n])
-        for c in range(len(CHUNKS)):
-            sent = [(R_CORE, csend[c]), (R_PRS, plr[c]), (R_PAG, plr[c]), (R_CAG, GA[c])]
-            if direct(c):
-                sent += [(R_A0, axb[c]), (R_G0, axb[c])]
-            else:
-                sent += [(R_A0, axa[c].at[0]), (R_A1, axa[c].at[1]), (R_B0, axb[c].at[0]), (R_B1, axb[c].at[1])]
-                sent += [(R_G0, axb[c].at[0]), (R_G1, axb[c].at[1]), (R_H0, axa[c].at[0]), (R_H1, axa[c].at[1])]
-            for n, ref in sent:
-                landed(ref, csem.at[c, n])
-            pltpu.make_async_copy(GA[c], big_hbm[c].at[core], osem.at[2 * c]).wait()
-            pltpu.make_async_copy(GB[c], big_hbm[c].at[1 - core], osem.at[2 * c + 1]).wait()
-        landed(dpr, ssend.at[0])
-        landed(dpr.at[0:3], ssend.at[1])
+        drain(range(len(CHUNKS)), (R_G0, R_G1, R_H0, R_H1, R_CAG))
         landed(dpr, ssend.at[2])
-        pltpu.make_async_copy(dout, small_hbm, osem.at[OUT]).wait()
-        for part in (0, 1):
-            rows = slice(part * 512, part * 512 + 512)
-            pltpu.make_async_copy(obuf.at[rows], gin_hbm.at[rows], osem.at[OUT + 1 + part]).wait()
 
 
 def finish_kernel(*refs):
     refs = list(refs)
     n_ch = len(CHUNKS)
-    gin_hbm, small_hbm = refs[:2]
-    big_hbm = refs[2 : 2 + n_ch]
-    gout_hbm, dw_hbm, gain_hbm, up_hbm, down_hbm, gbuf, sbuf, dbuf, kbuf = refs[2 + n_ch : 11 + n_ch]
-    narrow = refs[11 + n_ch : 11 + 2 * n_ch]
-    downs = refs[11 + 2 * n_ch : 11 + 3 * n_ch]
-    ups = refs[11 + 3 * n_ch : 11 + 4 * n_ch]
-    isem, osem = refs[11 + 4 * n_ch :]
-    ins = [
-        [pltpu.make_async_copy(big_hbm[c].at[s], narrow[c].at[s], isem.at[2 * c + s]) for s in range(2)]
-        for c in range(n_ch)
-    ]
-    for pair in ins:
-        for c_ in pair:
-            c_.start()
-    first = pltpu.make_async_copy(gin_hbm, gbuf, isem.at[2 * n_ch])
-    second = pltpu.make_async_copy(small_hbm, sbuf, isem.at[2 * n_ch + 1])
-    first.start()
-    second.start()
+    gin, small = refs[:2]
+    own, other = refs[2 : 2 + n_ch], refs[2 + n_ch : 2 + 2 * n_ch]
+    gout_hbm, dw_hbm, gain_hbm, up_hbm, down_hbm, dbuf, kbuf = refs[2 + 2 * n_ch : 9 + 2 * n_ch]
+    downs, ups = refs[9 + 2 * n_ch : 9 + 3 * n_ch], refs[9 + 3 * n_ch : 9 + 4 * n_ch]
+    osem = refs[-1]
     outs = []
 
     def put(src, dst):
         outs.append(pltpu.make_async_copy(src, dst, osem.at[len(outs)]))
         outs[-1].start()
 
-    for c, w in enumerate(CHUNKS):
-        half = w // 2
-        for s in range(2):
-            ins[c][s].wait()
-            wide = (downs, ups)[s][c]
+    def widen(c, down, up):
+        half = CHUNKS[c] // 2
+        for narrow, wide in ((down, downs[c]), (up, ups[c])):
             rows = wide.shape[0]
-            step = min(rows, 1024) // 4
+            step = rows // 4
 
             @pl.loop(0, 4)
             def _(t):
                 rs = pl.ds(pl.multiple_of(t * step, step), step)
                 for n in range(1024 // rows):
-                    wide[rs, n * half : (n + 1) * half] = narrow[c][
-                        s, pl.ds(pl.multiple_of(n * rows + t * step, step), step), :
+                    wide[rs, n * half : (n + 1) * half] = narrow[
+                        pl.ds(pl.multiple_of(n * rows + t * step, step), step), :
                     ].astype(F32)
 
-            part = pl.ds(STARTS[c], w)
-            put(wide, down_hbm.at[part] if s == 0 else up_hbm.at[:, part])
-    first.wait()
-    put(gbuf, gout_hbm)
-    second.wait()
-    dbuf[...] = sbuf[0:49, :]
-    kbuf[...] = sbuf[49:50, :]
+    core = lax.axis_index("rows") % 2
+    for c, w in enumerate(CHUNKS):
+        @pl.when(core == 0)
+        def _():
+            widen(c, own[c], other[c])
+
+        @pl.when(core == 1)
+        def _():
+            widen(c, other[c], own[c])
+
+        part = pl.ds(STARTS[c], w)
+        put(downs[c], down_hbm.at[part])
+        put(ups[c], up_hbm.at[:, part])
+    put(gin, gout_hbm)
+    dbuf[...] = small[0:49, :]
+    kbuf[...] = small[49:50, :]
     put(dbuf, dw_hbm)
     put(kbuf, gain_hbm)
     for c_ in outs:
@@ -687,7 +700,7 @@
 
 def finish(gin, small, big):
     vm, dma = pltpu.VMEM, pltpu.SemaphoreType.DMA
-    any_ = pl.BlockSpec(memory_space=pl.ANY)
+    any_, here = pl.BlockSpec(memory_space=pl.ANY), pl.BlockSpec(memory_space=pltpu.VMEM)
     n_ch = len(CHUNKS)
     gin, dw, gain, up, down = pl.pallas_call(
         finish_kernel,
@@ -698,16 +711,15 @@
             jax.ShapeDtypeStruct((CH, FF), F32),
             jax.ShapeDtypeStruct((FF, CH), F32),
         ),
-        in_specs=[any_] * (2 + n_ch),
+        in_specs=[here] * (2 + 2 * n_ch),
         out_specs=[any_] * 5,
-        scratch_shapes=[vm((PIX, CH), BF16), vm((64, CH), F32), vm((49, CH), F32), vm((1, CH), F32)]
-        + [vm((2, 1024, w // 2), BF16) for w in CHUNKS]
+        scratch_shapes=[vm((49, CH), F32), vm((1, CH), F32)]
         + [vm((w, CH), F32) for w in CHUNKS]
         + [vm((CH, w), F32) for w in CHUNKS]
-        + [dma((2 * n_ch + 2,)), dma((2 * n_ch + 3,))],
-        compiler_params=pltpu.CompilerParams(vmem_limit_bytes=66_000_000),
+        + [dma((2 * n_ch + 3,))],
+        compiler_params=pltpu.CompilerParams(vmem_limit_bytes=24_000_000),
         name="finish",
-    )(gin, small, *[b.reshape(2, 1024, w // 2) for b, w in zip(big, CHUNKS)])
+    )(gin, small, *[b.reshape(1024, w // 2) for b, w in zip(big, CHUNKS * 2)])
     return gin.reshape(ROWS, COLS, CH), dw, gain.reshape(CH), up, down
 
 
@@ -721,33 +733,34 @@
         whole = vm((4, 16, 16, h), BF16)
         comm += [vm((2, 1024, h), F32), whole, whole, whole]
         comm += [vm((2, 8, 16, h), BF16), vm((2, 16, 16, h), BF16), vm((3 if direct(c) else 2, 16, 16, h), BF16)]
-        comm += [vm((16, 16, h), BF16), vm((15, 16, h), BF16), whole, whole]
+        comm += [vm((16, 16, h), BF16), vm((15, 16, h), BF16)]
     gin, small, *big = pl.pallas_call(
         kernel,
         out_shape=(
-            jax.ShapeDtypeStruct((PIX, CH), BF16),
-            jax.ShapeDtypeStruct((64, CH), F32),
-            *[jax.ShapeDtypeStruct((2, 4, 16, 16, w // 2), BF16) for w in CHUNKS],
+            vm((PIX, CH), BF16),
+            vm((64, CH), F32),
+            *[vm((4, 16, 16, w // 2), BF16) for w in CHUNKS * 2],
         ),
         in_specs=[any_] * 6,
-        out_specs=[any_] * (2 + n_ch),
+        out_specs=[pl.BlockSpec(memory_space=pltpu.VMEM)] * (2 + 2 * n_ch),
         scratch_shapes=[
             vm((ROWS, COLS, CH), BF16), vm((PIX, CH), BF16), vm((CH, FF), BF16), vm((FF, CH), BF16),
             vm((49, CH), F32), vm((1, CH), F32),
             vm((4, 14, 144, 128), F32), vm((4, 14, 144, 128), F32), vm((4, 49, 8, 128), F32),
             vm((4, PIX, 128), F32), vm((4, PIX, 128), F32), vm((PIX, 128), F32), vm((PIX, CH), BF16),
             vm((PIX, max(CHUNKS)), BF16), vm((PIX, FF), BF16), vm((PIX, CH), F32),
-            vm((ROWS, COLS, CH), BF16), vm((PIX, CH), BF16),
+            vm((ROWS, COLS, CH), BF16),
             vm((2, 2, 8, 8, CH), BF16), vm((2, 2, 3, COLS, CH), BF16), vm((2, 2, 8, 8, CH), BF16), vm((2, 4, 3, 8, CH), BF16),
             vm((4, 64, 128), F32), vm((32, 8, 128), F32), vm((31, 8, 128), F32), vm((4, 8, 128), F32),
-            vm((32, 8, 128), F32), vm((64, CH), F32),
+            vm((32, 8, 128), F32),
         ]
         + comm
         + [
-            dma((6,)), dma((2, 8)), dma((2, 8)), dma((n_ch, 12)), dma((n_ch, 12)), dma((3,)), dma((3,)), dma((2 * n_ch + 3,)),
+            dma((6,)), dma((2, 8)), dma((2, 8)), dma((n_ch, 12)), dma((n_ch, 12)), dma((3,)), dma((3,)),
+            pltpu.SemaphoreType.REGULAR((4,)),
         ],
         compiler_params=pltpu.CompilerParams(
-            collective_id=0, has_side_effects=True, vmem_limit_bytes=67_000_000
+            collective_id=0, has_side_effects=True, vmem_limit_bytes=58_000_000
         ),
         name="block_backward",
     )(features, dw_weight, norm_gain.reshape(1, CH), w_up, w_down, cotangent.reshape(PIX, CH))

time: 77.7 us -> 73.8 us (0.950)
  Pallas kernels: 76.8 us -> 72.9 us
    pallas_call x1, Pallas kernels: 71.8 us -> 68.9 us  [on_device(): pl.pallas_call(kernel, out_shape=(vm((PIX, CH), BF16), vm((64, CH), F32),...]
    pallas_call x1, Pallas kernels: 4.95 us -> 3.91 us  [finish(): pl.pallas_call(finish_kernel, out_shape=(jax.ShapeDtypeStruct((PIX, CH),...]
where the time goes in v3:
time: 73.8 us; the launch traced here: 73.7 us
  Pallas kernels  72.9 us (99%)
  between operations  0.8 us (1%)
    pallas_call x1, Pallas kernels, on_device(): pl.pallas_call(kernel, out_shape=(vm((PIX, CH), BF16), vm((64, CH), F32),...  68.9 us
    pallas_call x1, Pallas kernels, finish(): pl.pallas_call(finish_kernel, out_shape=(jax.ShapeDtypeStruct((PIX, CH),...  3.91 us

profile of v3, /device:TPU:1, one launch (start us, length us, event | category | flops | bytes accessed | tf_op | source)
XLA Modules:
  0.0 73.7 jit_solution(12420113174564675275)
XLA Ops:
  0.6 68.9 %block_backward.1 = (bf16[1024,512]{1,0:T(8,128)(2,1)S(1)}, f32[64,512]{1,0:T(8,128)S(1)}, bf16[4,16,16,256]{3,2,1,0:T(8,128)(2,1)S(1)}, bf16[4,16,16,256]{3,2,1...) custom-call(bf16[8,128,512]{2,1,0:T(8,128)(2,1)} %refs_0_.1, ...), custom_call_target="tpu_custom_call" | custom-call | tf_op jit(solution)/shard_map/block_backward/pallas_call | solution.py:737
  69.6 3.9 %finish.1 = (bf16[1024,512]{1,0:T(8,128)(2,1)}, f32[49,512]{1,0:T(8,128)}, f32[1,512]{1,0:T(1,128)}, f32[512,2048]{1,0:T(8,128)}, f32[2048,512]{1,0:T(8,128)}) custom-call(bf16[1024,512]{1,0:T(8,128)(2,1)S(1)} %get-tuple-element.22.refs_0_, f32[64,512]{1,0:T(8,128)S(1)} %get-tuple-element.23.refs_1_, bf16[1024,256]{1,0:T(8,128)(2,1)S(1)} %bitcast.14, ...), custom_call_target="tpu_custom_call" | custom-call | tf_op jit(solution)/shard_map/finish/pallas_call | solution.py:705

commit v4 on v3

--- a/solution.py
+++ b/solution.py
@@ -33,7 +33,7 @@
     feat_hbm, dww_hbm, gain_hbm, wup_hbm, wdn_hbm, cot_hbm = take(6)
     obuf, dout = take(2)
     GA, GB = take(len(CHUNKS)), take(len(CHUNKS))
-    fbuf, cbuf, wup, wdn, dww, gainb, xf, gp, wb, cv, nv, invb, sc = take(13)
+    fbuf, cbuf, wup, wdn, dww, gainb, xf, gp, wb, cv, nv, invb, sc, sct = take(14)
     act, gh, gs, gb, scol, hrow, hcol, hcor = take(8)
     gd, dsm, dpr, dax, dga = take(5)
     G, csend, crecv, M, axa, axs, axb, pls, plr = zip(*[take(9) for _ in CHUNKS])
@@ -200,20 +200,19 @@
                     phase, n - 4, :, :, cc * 128 : cc * 128 + 128
                 ].astype(F32) * (valid[dr] * valid_c[dc])
 
-    def conv(pad, flip, cc, cb, inner):
+    def conv(pad, flip, cc, starts, inner):
         rhos = range(3, 11) if inner else (0, 1, 2, 11, 12, 13)
         rows = range(ROWS) if inner else (0, 1, 2, 5, 6, 7)
-        base = cb * 32
 
         def at(r, b):
-            return pl.ds(pl.multiple_of(r * COLS + base + 8 * b, 8), 8)
+            return pl.ds(pl.multiple_of(r * COLS + starts[b], 8), 8)
 
         def body(j, acc):
             acc = dict(zip([(r, b) for r in rows for b in range(4)], acc))
             w = [wb[cc, (48 - 7 * i - j) if flip else (7 * i + j)] for i in range(7)]
             for rho in rhos:
                 for b in range(4):
-                    v = pad[cc, rho, pl.ds(base + (8 * b + LEFT - 3) + j, 8), :]
+                    v = pad[cc, rho, pl.ds(starts[b] + (LEFT - 3) + j, 8), :]
                     for r in rows:
                         if 0 <= rho - r <= 6:
                             acc[r, b] = acc[r, b] + v * w[rho - r]
@@ -227,6 +226,9 @@
         for n, (r, b) in enumerate([(r, b) for r in rows for b in range(4)]):
             cv[cc, at(r, b), :] = acc[n]
 
+    def groups(base):
+        return [base + 8 * b for b in range(4)]
+
     halo = halo_copies(0, fbuf)
     with jax.named_scope("taps"):
         for n in (2, 3, 0, 1, 4, 5, 6, 7):
@@ -237,9 +239,9 @@
                 wb[cc, t] = jnp.broadcast_to(dww[t : t + 1, cc * 128 : cc * 128 + 128], (8, 128))
 
     with jax.named_scope("fconv_mid"):
-        @pl.loop(0, 8)
+        @pl.loop(0, 12)
         def _(t):
-            conv(xf, False, t // 2, 1 + t % 2, True)
+            conv(xf, False, t // 3, groups(8 + 32 * (t % 3)), True)
 
     with jax.named_scope("fhalo_c"):
         round_wait(0)
@@ -247,9 +249,9 @@
         halo_cols(0, xf)
 
     with jax.named_scope("fconv_side"):
-        @pl.loop(0, 8)
+        @pl.loop(0, 4)
         def _(t):
-            conv(xf, False, t // 2, 3 * (t % 2), True)
+            conv(xf, False, t, (0, 104, 112, 120), True)
 
     with jax.named_scope("fhalo_r"):
         round_wait(1)
@@ -259,7 +261,7 @@
     with jax.named_scope("fconv_out"):
         @pl.loop(0, 16)
         def _(t):
-            conv(xf, False, t // 4, t % 4, False)
+            conv(xf, False, t // 4, groups(32 * (t % 4)), False)
 
     round_wait(2)
     round_signal(3)
@@ -307,8 +309,15 @@
 
     def mlp_up(c):
         fs = slice(STARTS[c], STARTS[c] + CHUNKS[c])
-        put(c, 1 - core, lax.dot_general(
-            sc[...], gh[:, fs], (((0,), (0,)), ((), ())), preferred_element_type=F32))
+        if CHUNKS[c] < 512:
+            for n in range(2):
+                rs = slice(n * 256, n * 256 + 256)
+                v = jnp.dot(sct[rs, :], gh[:, fs], preferred_element_type=F32)
+                w = CHUNKS[c] // 2
+                for k in range(2):
+                    G[c][1 - core, k * 512 + n * 256 : k * 512 + n * 256 + 256, :] = v[:, k * w : (k + 1) * w]
+        else:
+            put(c, 1 - core, jnp.dot(sct[...], gh[:, fs], preferred_element_type=F32))
 
     def mlp_back(q):
         ps = slice(q * 256, q * 256 + 256)
@@ -375,7 +384,7 @@
             total = total + axb[c][n].astype(F32)
         pls[c][...] = total.astype(BF16)
 
-        @pl.loop(1, 16, unroll=5)
+        @pl.loop(1, 16, unroll=15)
         def _(d):
             to, pos = plane_peer(d, axis)
             send(c, R_PRS, pls[c].at[pos], plr[c].at[d - 1], to)
@@ -389,7 +398,7 @@
             total = total + plr[c][d].astype(F32)
         GA[c][p, pos] = total.astype(BF16)
 
-        @pl.loop(1, 16, unroll=5)
+        @pl.loop(1, 16, unroll=15)
         def _(d):
             to, _ = plane_peer(d, axis)
             send(c, R_PAG, GA[c].at[p, pos], GA[c].at[p, pos], to)
@@ -498,7 +507,7 @@
             for tb in range(8):
                 dsm[8 * cc + tb] = gd[cc, 8 * tb : 8 * tb + 8, :]
 
-        @pl.loop(1, 32)
+        @pl.loop(1, 32, unroll=31)
         def _(d):
             to, pos = pair_peer(d)
             remote(dsm.at[pos], dpr.at[d - 1], ssend.at[0], srecv.at[0], to).start()
@@ -516,7 +525,7 @@
         landed(dpr.at[0:3], srecv.at[1])
         dga[mine] = dax[0] + dax[1] + dax[2] + dax[3]
 
-        @pl.loop(1, 32)
+        @pl.loop(1, 32, unroll=31)
         def _(d):
             to, _ = pair_peer(d)
             remote(dga.at[mine], dga.at[mine], ssend.at[2], srecv.at[2], to).start()
@@ -530,12 +539,12 @@
     def gin_inner(cb, half):
         @pl.loop(2 * half, 2 * half + 2)
         def _(t):
-            conv(gp, True, t, cb, True)
+            conv(gp, True, t, groups(32 * cb), True)
 
     def gin_outer(cb):
         @pl.loop(0, 4)
         def _(t):
-            conv(gp, True, t, cb, False)
+            conv(gp, True, t, groups(32 * cb), False)
 
     def gin_store(part):
         @pl.loop(part * 8, part * 8 + 8)
@@ -549,6 +558,8 @@
         for q in range(5):
             if q < 4:
                 norm(q)
+                qs = slice(q * 256, q * 256 + 256)
+                sct[:, qs] = sc[qs, :].T
             if q > 0:
                 mlp_a(0, (q - 1,))
 
@@ -572,6 +583,8 @@
                 (0.0, ch_core), (2.5, ch_axis), (4.0, ch_axis2), (5.0, ch_plane), (7.0, ch_share),
                 (6.0, ch_back), (5.0, ch_back2), (5.0, ch_pair), (2.5, ch_end),
             )
+        more = {(2, ch_back): 1.8}
+        steps = tuple((gap + more.get((c, fn), 0.0), fn) for gap, fn in steps)
         chains[c] = [((0.85 if n < 4 else 0.85) * gap, fn.__name__, lambda fn=fn, c=c: fn(c)) for n, (gap, fn) in enumerate(steps)]
     def both(q):
         if q < 4:
@@ -747,7 +760,7 @@
             vm((ROWS, COLS, CH), BF16), vm((PIX, CH), BF16), vm((CH, FF), BF16), vm((FF, CH), BF16),
             vm((49, CH), F32), vm((1, CH), F32),
             vm((4, 14, 144, 128), F32), vm((4, 14, 144, 128), F32), vm((4, 49, 8, 128), F32),
-            vm((4, PIX, 128), F32), vm((4, PIX, 128), F32), vm((PIX, 128), F32), vm((PIX, CH), BF16),
+            vm((4, PIX, 128), F32), vm((4, PIX, 128), F32), vm((PIX, 128), F32), vm((PIX, CH), BF16), vm((CH, PIX), BF16),
             vm((PIX, max(CHUNKS)), BF16), vm((PIX, FF), BF16), vm((PIX, CH), F32),
             vm((ROWS, COLS, CH), BF16),
             vm((2, 2, 8, 8, CH), BF16), vm((2, 2, 3, COLS, CH), BF16), vm((2, 2, 8, 8, CH), BF16), vm((2, 4, 3, 8, CH), BF16),

time: 73.8 us -> 71.7 us (0.972)
  Pallas kernels: 72.9 us -> 70.7 us
    pallas_call x1, Pallas kernels: 68.9 us -> 66.8 us  [on_device(): pl.pallas_call(kernel, out_shape=(vm((PIX, CH), BF16), vm((64, CH), F32),...]
where the time goes in v4:
time: 71.7 us; the launch traced here: 71.5 us
  Pallas kernels  70.7 us (99%)
  between operations  0.8 us (1%)
    pallas_call x1, Pallas kernels, on_device(): pl.pallas_call(kernel, out_shape=(vm((PIX, CH), BF16), vm((64, CH), F32),...  66.8 us
    pallas_call x1, Pallas kernels, finish(): pl.pallas_call(finish_kernel, out_shape=(jax.ShapeDtypeStruct((PIX, CH),...  3.91 us

profile of v4, /device:TPU:1, one launch (start us, length us, event | category | flops | bytes accessed | tf_op | source)
XLA Modules:
  0.0 71.5 jit_solution(13967496773266486606)
XLA Ops:
  0.6 66.8 %block_backward.1 = (bf16[1024,512]{1,0:T(8,128)(2,1)S(1)}, f32[64,512]{1,0:T(8,128)S(1)}, bf16[4,16,16,256]{3,2,1,0:T(8,128)(2,1)S(1)}, bf16[4,16,16,256]{3,2,1...) custom-call(bf16[8,128,512]{2,1,0:T(8,128)(2,1)} %refs_0_.1, ...), custom_call_target="tpu_custom_call" | custom-call | tf_op jit(solution)/shard_map/block_backward/pallas_call | solution.py:750
  67.5 3.9 %finish.1 = (bf16[1024,512]{1,0:T(8,128)(2,1)}, f32[49,512]{1,0:T(8,128)}, f32[1,512]{1,0:T(1,128)}, f32[512,2048]{1,0:T(8,128)}, f32[2048,512]{1,0:T(8,128)}) custom-call(bf16[1024,512]{1,0:T(8,128)(2,1)S(1)} %get-tuple-element.22.refs_0_, f32[64,512]{1,0:T(8,128)S(1)} %get-tuple-element.23.refs_1_, bf16[1024,256]{1,0:T(8,128)(2,1)S(1)} %bitcast.14, ...), custom_call_target="tpu_custom_call" | custom-call | tf_op jit(solution)/shard_map/finish/pallas_call | solution.py:718

commit v5 on v4

--- a/solution.py
+++ b/solution.py
@@ -689,6 +689,11 @@
                         pl.ds(pl.multiple_of(n * rows + t * step, step), step), :
                     ].astype(F32)
 
+    put(gin, gout_hbm)
+    dbuf[...] = small[0:49, :]
+    kbuf[...] = small[49:50, :]
+    put(dbuf, dw_hbm)
+    put(kbuf, gain_hbm)
     core = lax.axis_index("rows") % 2
     for c, w in enumerate(CHUNKS):
         @pl.when(core == 0)
@@ -702,11 +707,6 @@
         part = pl.ds(STARTS[c], w)
         put(downs[c], down_hbm.at[part])
         put(ups[c], up_hbm.at[:, part])
-    put(gin, gout_hbm)
-    dbuf[...] = small[0:49, :]
-    kbuf[...] = small[49:50, :]
-    put(dbuf, dw_hbm)
-    put(kbuf, gain_hbm)
     for c_ in outs:
         c_.wait()
 

time: 71.7 us -> 71.5 us (level)
  no operation moved by 1% of the time
where the time goes in v5:
time: 71.5 us; the launch traced here: 71.4 us
  Pallas kernels  70.6 us (99%)
  between operations  0.8 us (1%)
    pallas_call x1, Pallas kernels, on_device(): pl.pallas_call(kernel, out_shape=(vm((PIX, CH), BF16), vm((64, CH), F32),...  66.8 us
    pallas_call x1, Pallas kernels, finish(): pl.pallas_call(finish_kernel, out_shape=(jax.ShapeDtypeStruct((PIX, CH),...  3.76 us

profile of v5, /device:TPU:1, one launch (start us, length us, event | category | flops | bytes accessed | tf_op | source)
XLA Modules:
  0.0 71.4 jit_solution(2975339826411176602)
XLA Ops:
  0.6 66.8 %block_backward.1 = (bf16[1024,512]{1,0:T(8,128)(2,1)S(1)}, f32[64,512]{1,0:T(8,128)S(1)}, bf16[4,16,16,256]{3,2,1,0:T(8,128)(2,1)S(1)}, bf16[4,16,16,256]{3,2,1...) custom-call(bf16[8,128,512]{2,1,0:T(8,128)(2,1)} %refs_0_.1, ...), custom_call_target="tpu_custom_call" | custom-call | tf_op jit(solution)/shard_map/block_backward/pallas_call | solution.py:750
  67.5 3.8 %finish.1 = (bf16[1024,512]{1,0:T(8,128)(2,1)}, f32[49,512]{1,0:T(8,128)}, f32[1,512]{1,0:T(1,128)}, f32[512,2048]{1,0:T(8,128)}, f32[2048,512]{1,0:T(8,128)}) custom-call(bf16[1024,512]{1,0:T(8,128)(2,1)S(1)} %get-tuple-element.22.refs_0_, f32[64,512]{1,0:T(8,128)S(1)} %get-tuple-element.23.refs_1_, bf16[1024,256]{1,0:T(8,128)(2,1)S(1)} %bitcast.14, ...), custom_call_target="tpu_custom_call" | custom-call | tf_op jit(solution)/shard_map/finish/pallas_call | solution.py:718
